TPU v7x, 512 devices: a whole 4x4x16 slice. The times are simulated.
512 devices in a mesh: tm: 4 (over y), row: 16 (over z), col: 8 (over x, core).
Axes of the slice: x: 4, y: 4, z: 16, core: 2. Of those that a mesh axis runs over, the one named last changes fastest.
Arguments:
- noisy_video: float32 [16, 2048, 2048], P('tm', 'row', 'col'), may hold values from -6 to 6
- fidelity: float32 [16, 2048, 2048], P('tm', 'row', 'col'), may hold values from 0.5 to 12, as said below
Outputs:
- denoised: float32 [16, 2048, 2048], P('tm', 'row', 'col')
- gaps: float32 [3], replicated
Inputs may be any that keep to these rules, and one draw needn't show every extreme that they name: `fidelity`: positive, larger on average toward later rows.
All inputs are finite; a program needn't handle non-finite values.
Results may differ from a plain program's by a relative error of at most 0.0001.
Values sent between devices are 32-bit elements; how exact they have to be, the bound alone decides.
No kernel may reach another device: no remote copies, remote signals or barrier semaphores. Data moves between devices by JAX's collectives and lax.ppermute only.
A program may use at most 64 MiB of HBM per device.

v0:
```python
import jax
import jax.numpy as jnp
from jax import lax
from jax.sharding import Mesh
from jax.sharding import PartitionSpec as P

ITERS = 3
COL = ("col_0", "col_1")
TM_ROW_COL = ("tm", "row", "col_0", "col_1")


sigma_step = 0.28
tau_step = 0.28


def shifted(block, axis, distance):
    devices = range(lax.axis_size(axis))
    route = [(i - distance, i) for i in devices if i - distance in devices]
    return lax.ppermute(block, axis, route)


def one_axis_at_a_time(value, axes):
    for axis in axes:
        value = lax.psum(value, axis)
    return value


def ahead_diff(field, ghost, axis, is_last):
    count = field.shape[axis]
    inner = lax.slice_in_dim(field, 1, count, axis=axis)
    own_last = lax.slice_in_dim(field, count - 1, count, axis=axis)
    following = jnp.concatenate([inner, jnp.where(is_last, own_last, ghost)], axis=axis)
    return following - field


def behind_diff(comp, ghost, axis):
    count = comp.shape[axis]
    before = jnp.concatenate([ghost, lax.slice_in_dim(comp, 0, count - 1, axis=axis)], axis=axis)
    return comp - before


def project(duals, grads):
    moved_time = duals[0] + sigma_step * grads[0]
    moved_rows = duals[1] + sigma_step * grads[1]
    moved_cols = duals[2] + sigma_step * grads[2]
    length = jnp.sqrt(moved_time * moved_time + moved_rows * moved_rows + moved_cols * moved_cols)
    scale = jnp.maximum(1.0, length)
    return [moved_time / scale, moved_rows / scale, moved_cols / scale]


def on_device(noisy_video, fidelity):
    frames, rows_dev, cols_dev = noisy_video.shape
    cells = float(
        noisy_video.size * lax.axis_size("tm") * lax.axis_size("row") * lax.axis_size(COL)
    )
    last_frame = lax.axis_index("tm") == lax.axis_size("tm") - 1
    last_row = lax.axis_index("row") == lax.axis_size("row") - 1
    last_col = lax.axis_index(COL) == lax.axis_size(COL) - 1
    field = noisy_video
    ubar_field = noisy_video
    zero_dual = jnp.zeros_like(noisy_video)
    duals = [zero_dual, zero_dual, zero_dual]
    grad_u = None
    local_gaps = []
    for iteration in range(ITERS):
        ghost_time = shifted(ubar_field[0:1], "tm", -1)
        ghost_rows = shifted(ubar_field[:, 0:1], "row", -1)
        ghost_cols = shifted(ubar_field[:, :, 0:1], COL, -1)
        grads = [
            ahead_diff(ubar_field, ghost_time, 0, last_frame),
            ahead_diff(ubar_field, ghost_rows, 1, last_row),
            ahead_diff(ubar_field, ghost_cols, 2, last_col),
        ]
        duals = project(duals, grads)
        prev_time = shifted(duals[0][frames - 1 :], "tm", 1)
        prev_rows = shifted(duals[1][:, rows_dev - 1 :], "row", 1)
        prev_cols = shifted(duals[2][:, :, cols_dev - 1 :], COL, 1)
        diverge = (
            behind_diff(duals[0], prev_time, 0)
            + behind_diff(duals[1], prev_rows, 1)
            + behind_diff(duals[2], prev_cols, 2)
        )
        if iteration == 0:
            grad_u = grads
        else:
            grad_u = [
                0.5 * (grads[0] + grad_u[0]),
                0.5 * (grads[1] + grad_u[1]),
                0.5 * (grads[2] + grad_u[2]),
            ]
        total_var = jnp.sqrt(grad_u[0] * grad_u[0] + grad_u[1] * grad_u[1] + grad_u[2] * grad_u[2])
        resid = field - noisy_video
        term = (
            0.5 * fidelity * resid * resid
            + total_var
            + diverge * diverge / (2.0 * fidelity)
            + noisy_video * diverge
        )
        local_sum = jnp.sum(term)
        local_gaps.append(local_sum)
        new_field = (field + tau_step * diverge + tau_step * fidelity * noisy_video) / (
            1.0 + tau_step * fidelity
        )
        ubar_field = 2.0 * new_field - field
        field = new_field
    gaps = one_axis_at_a_time(jnp.stack(local_gaps), TM_ROW_COL) / cells
    return (field, gaps)


def solution(mesh):
    finer = Mesh(
        mesh.devices.reshape(mesh.shape["tm"], mesh.shape["row"], 4, 2),
        ("tm", "row", "col_0", "col_1"),
    )
    placed = (P("tm", "row", COL), P("tm", "row", COL))
    return jax.shard_map(
        on_device,
        mesh=finer,
        in_specs=placed,
        out_specs=(P("tm", "row", COL), P()),
        check_vma=False,
    )
```

profile of v0, /device:TPU:1, one launch (start us, length us, event | category | flops | bytes accessed | tf_op | source)
XLA Modules:
  0.0 153.8 jit_solution(11274911746246239184)
XLA Ops:
  1.7 8.7 %collective-permute-start.2 = (f32[4,128,1]{2,1,0:T(8,128)S(1)}, f32[4,128,1]{2,1,0:T(8,128)S(1)}, u32[]{:S(2)}, u32[]{:S(2)}) collective-permute-start(f32[4,128,1]{2,1,0:T(8,128)S(1)} %slice.143), channel_id=1, source_target_pairs={{1,0},{2,1},{3,2},{4,3},{5,4},{6,5},{7,6},{9,8},{10,9},{11,10},{12... | collective-permute-start | bytes 6152 | tf_op jit(solution)/shard_map/ppermute | solution.py:19
  10.5 1.3 collective-permute-start.1
  13.5 1.4 collective-permute-done.1
  15.0 3.9 %collective-permute-done = f32[1,128,256]{2,1,0:T(8,128)S(1)} collective-permute-done((f32[1,128,256]{2,1,0:T(8,128)S(1)}, f32[1,128,256]{2,1,0:T(8,128)S(1)}, u32[]{:S(2)}, u32[]{:S(2)}) %collective-permute-start) | collective-permute-done | bytes 131104 | tf_op jit(solution)/shard_map/ppermute | solution.py:19
  19.4 1.4 collective-permute-start.3
  20.8 4.1 %collective-permute-start.4 = (f32[4,1,256]{2,1,0:T(1,128)S(1)}, f32[4,1,256]{2,1,0:T(1,128)S(1)}, u32[]{:S(2)}, u32[]{:S(2)}) collective-permute-start(f32[4,1,256]{2,1,0:T(1,128)S(1)} %slice.182), channel_id=1, source_target_pairs={{0,8},{8,16},{16,24},{24,32},{32,40},{40,48},{48,56},{56,64},{64,7... | collective-permute-start | bytes 12296 | tf_op jit(solution)/shard_map/ppermute | solution.py:19
  25.0 2.1 %collective-permute-start.5 = (f32[4,128,1]{2,1,0:T(8,128)S(1)}, f32[4,128,1]{2,1,0:T(8,128)S(1)}, u32[]{:S(2)}, u32[]{:S(2)}) collective-permute-start(f32[4,128,1]{2,1,0:T(8,128)S(1)} %slice.184), channel_id=1, source_target_pairs={{0,1},{1,2},{2,3},{3,4},{4,5},{5,6},{6,7},{8,9},{9,10},{10,11},{11... | collective-permute-start | bytes 6152 | tf_op jit(solution)/shard_map/ppermute | solution.py:19
  27.1 3.3 %collective-permute-done.5 = f32[4,128,1]{2,1,0:T(8,128)S(1)} collective-permute-done((f32[4,128,1]{2,1,0:T(8,128)S(1)}, f32[4,128,1]{2,1,0:T(8,128)S(1)}, u32[]{:S(2)}, u32[]{:S(2)}) %collective-permute-start.5) | collective-permute-done | bytes 2080 | tf_op jit(solution)/shard_map/ppermute | solution.py:19
  30.9 1.9 %collective-permute-start.8 = (f32[4,128,1]{2,1,0:T(8,128)S(1)}, f32[4,128,1]{2,1,0:T(8,128)S(1)}, u32[]{:S(2)}, u32[]{:S(2)}) collective-permute-start(f32[4,128,1]{2,1,0:T(8,128)S(1)} %slice.194), channel_id=1, source_target_pairs={{1,0},{2,1},{3,2},{4,3},{5,4},{6,5},{7,6},{9,8},{10,9},{11,10},{12... | collective-permute-start | bytes 6152 | tf_op jit(solution)/shard_map/ppermute | solution.py:19
  33.1 1.3 collective-permute-start.7
  34.4 1.3 collective-permute-start.6
  35.7 3.6 %collective-permute-done.8 = f32[4,128,1]{2,1,0:T(8,128)S(1)} collective-permute-done((f32[4,128,1]{2,1,0:T(8,128)S(1)}, f32[4,128,1]{2,1,0:T(8,128)S(1)}, u32[]{:S(2)}, u32[]{:S(2)}) %collective-permute-start.8) | collective-permute-done | bytes 2080 | tf_op jit(solution)/shard_map/ppermute | solution.py:19
  40.9 2.1 %collective-permute-start.9 = (f32[1,128,256]{2,1,0:T(8,128)S(1)}, f32[1,128,256]{2,1,0:T(8,128)S(1)}, u32[]{:S(2)}, u32[]{:S(2)}) collective-permute-start(f32[1,128,256]{2,1,0:T(8,128)S(1)} %slice.195), channel_id=1, source_target_pairs={{0,128},{128,256},{256,384},{1,129},{129,257},{257,385},{2,130},{1... | collective-permute-start | bytes 393224 | tf_op jit(solution)/shard_map/ppermute | solution.py:19
  43.0 4.2 %collective-permute-start.10 = (f32[4,1,256]{2,1,0:T(1,128)S(1)}, f32[4,1,256]{2,1,0:T(1,128)S(1)}, u32[]{:S(2)}, u32[]{:S(2)}) collective-permute-start(f32[4,1,256]{2,1,0:T(1,128)S(1)} %slice.197), channel_id=1, source_target_pairs={{0,8},{8,16},{16,24},{24,32},{32,40},{40,48},{48,56},{56,64},{64,7... | collective-permute-start | bytes 12296 | tf_op jit(solution)/shard_map/ppermute | solution.py:19
  47.3 7.0 %collective-permute-start.11 = (f32[4,128,1]{2,1,0:T(8,128)S(1)}, f32[4,128,1]{2,1,0:T(8,128)S(1)}, u32[]{:S(2)}, u32[]{:S(2)}) collective-permute-start(f32[4,128,1]{2,1,0:T(8,128)S(1)} %slice.199), channel_id=1, source_target_pairs={{0,1},{1,2},{2,3},{3,4},{4,5},{5,6},{6,7},{8,9},{9,10},{10,11},{11... | collective-permute-start | bytes 6152 | tf_op jit(solution)/shard_map/ppermute | solution.py:19
  54.4 3.3 %collective-permute-done.11 = f32[4,128,1]{2,1,0:T(8,128)S(1)} collective-permute-done((f32[4,128,1]{2,1,0:T(8,128)S(1)}, f32[4,128,1]{2,1,0:T(8,128)S(1)}, u32[]{:S(2)}, u32[]{:S(2)}) %collective-permute-start.11) | collective-permute-done | bytes 2080 | tf_op jit(solution)/shard_map/ppermute | solution.py:19
  57.7 1.9 %fusion.3 = (f32[]{:T(128)}, f32[]{:T(128)}, f32[4,128,256]{2,1,0:T(8,128)S(1)}) fusion(f32[4,128,256]{2,1,0:T(8,128)S(1)} %copy-done, f32[4,128,256]{2,1,0:T(8,128)S(1)} %get-tuple-element.17, f32[4,128,256]{2,1,0:T(8,128)S(1)} %copy-done.1, f32[1,128,256]{2,1,0:T(8,128)S(1)} %slice_select_fusion.5, f32[3,128,256]{2,1,0:T(8,128)S(1)} %slice.135, ...), kind=kLoop, calls=%fused_computation.6 | loop fusion | flops 7733246 | bytes 8388616 | tf_op jit(solution)/shard_map/reduce_sum | solution.py:99
  59.9 1.9 %collective-permute-start.14 = (f32[4,128,1]{2,1,0:T(8,128)S(1)}, f32[4,128,1]{2,1,0:T(8,128)S(1)}, u32[]{:S(2)}, u32[]{:S(2)}) collective-permute-start(f32[4,128,1]{2,1,0:T(8,128)S(1)} %slice.209), channel_id=1, source_target_pairs={{1,0},{2,1},{3,2},{4,3},{5,4},{6,5},{7,6},{9,8},{10,9},{11,10},{12... | collective-permute-start | bytes 6152 | tf_op jit(solution)/shard_map/ppermute | solution.py:19
  62.1 1.3 collective-permute-start.13
  63.4 1.3 collective-permute-start.12
  64.7 3.6 %collective-permute-done.14 = f32[4,128,1]{2,1,0:T(8,128)S(1)} collective-permute-done((f32[4,128,1]{2,1,0:T(8,128)S(1)}, f32[4,128,1]{2,1,0:T(8,128)S(1)}, u32[]{:S(2)}, u32[]{:S(2)}) %collective-permute-start.14) | collective-permute-done | bytes 2080 | tf_op jit(solution)/shard_map/ppermute | solution.py:19
  70.0 1.6 %collective-permute-start.15 = (f32[1,128,256]{2,1,0:T(8,128)S(1)}, f32[1,128,256]{2,1,0:T(8,128)S(1)}, u32[]{:S(2)}, u32[]{:S(2)}) collective-permute-start(f32[1,128,256]{2,1,0:T(8,128)S(1)} %slice.210), channel_id=1, source_target_pairs={{0,128},{128,256},{256,384},{1,129},{129,257},{257,385},{2,130},{1... | collective-permute-start | bytes 393224 | tf_op jit(solution)/shard_map/ppermute | solution.py:19
  71.7 4.5 %collective-permute-start.16 = (f32[4,1,256]{2,1,0:T(1,128)S(1)}, f32[4,1,256]{2,1,0:T(1,128)S(1)}, u32[]{:S(2)}, u32[]{:S(2)}) collective-permute-start(f32[4,1,256]{2,1,0:T(1,128)S(1)} %slice.212), channel_id=1, source_target_pairs={{0,8},{8,16},{16,24},{24,32},{32,40},{40,48},{48,56},{56,64},{64,7... | collective-permute-start | bytes 12296 | tf_op jit(solution)/shard_map/ppermute | solution.py:19
  76.3 6.7 %collective-permute-start.17 = (f32[4,128,1]{2,1,0:T(8,128)S(1)}, f32[4,128,1]{2,1,0:T(8,128)S(1)}, u32[]{:S(2)}, u32[]{:S(2)}) collective-permute-start(f32[4,128,1]{2,1,0:T(8,128)S(1)} %slice.214), channel_id=1, source_target_pairs={{0,1},{1,2},{2,3},{3,4},{4,5},{5,6},{6,7},{8,9},{9,10},{10,11},{11... | collective-permute-start | bytes 6152 | tf_op jit(solution)/shard_map/ppermute | solution.py:19
  83.1 3.3 %collective-permute-done.17 = f32[4,128,1]{2,1,0:T(8,128)S(1)} collective-permute-done((f32[4,128,1]{2,1,0:T(8,128)S(1)}, f32[4,128,1]{2,1,0:T(8,128)S(1)}, u32[]{:S(2)}, u32[]{:S(2)}) %collective-permute-start.17) | collective-permute-done | bytes 2080 | tf_op jit(solution)/shard_map/ppermute | solution.py:19
  86.3 2.8 %fusion.11 = (f32[]{:T(128)}, f32[4,128,256]{2,1,0:T(8,128)}) fusion(f32[4,128,256]{2,1,0:T(8,128)S(1)} %copy-done, f32[4,128,256]{2,1,0:T(8,128)S(1)} %get-tuple-element.9, f32[4,128,256]{2,1,0:T(8,128)S(1)} %get-tuple-element.10, f32[4,128,256]{2,1,0:T(8,128)S(1)} %copy-done.1, f32[4,128,256]{2,1,0:T(8,128)S(1)} %get-tuple-element.15, ...), kind=kLoop, calls=%fused_computation.14 | loop fusion | flops 7340031 | bytes 11010052 | tf_op jit(solution)/shard_map/reduce_sum | solution.py:99
  89.1 2.0 %pad_maximum_fusion = f32[3]{0:T(128)S(1)} fusion(f32[1]{0:T(128)} %bitcast.2, f32[1]{0:T(128)} %bitcast.1, f32[1]{0:T(128)} %bitcast), kind=kLoop, calls=%fused_computation.76 | loop fusion | flops 6 | bytes 24 | tf_op jit(solution)/shard_map/stack | solution.py:106
  91.1 6.0 %psum.28 = f32[3]{0:T(128)S(1)} all-reduce(f32[3]{0:T(128)S(1)} %pad_maximum_fusion), channel_id=1, replica_groups=mesh['tm'=4,'row'=16,'col_0'=4,'col_1'=2] {'tm'}, use_global_device_ids=true, to_apply=%region_3.4 | all-reduce | flops 3 | bytes 24 | tf_op jit(solution)/shard_map/psum | solution.py:24
  97.1 31.1 %psum.29 = f32[3]{0:T(128)S(1)} all-reduce(f32[3]{0:T(128)S(1)} %psum.28), channel_id=1, replica_groups=mesh['tm'=4,'row'=16,'col_0'=4,'col_1'=2] {'row'}, use_global_device_ids=true, to_apply=%region_4.5 | all-reduce | flops 3 | bytes 24 | tf_op jit(solution)/shard_map/psum | solution.py:24
  128.2 7.5 %psum.30 = f32[3]{0:T(128)S(1)} all-reduce(f32[3]{0:T(128)S(1)} %psum.29), channel_id=1, replica_groups=mesh['tm'=4,'row'=16,'col_0'=4,'col_1'=2] {'col_0'}, use_global_device_ids=true, to_apply=%region_5.6 | all-reduce | flops 3 | bytes 24 | tf_op jit(solution)/shard_map/psum | solution.py:24
  135.6 2.1 %add_divide_fusion = f32[4,128,256]{2,1,0:T(8,128)} fusion(f32[4,128,256]{2,1,0:T(8,128)} %get-tuple-element.6, f32[4,128,256]{2,1,0:T(8,128)S(1)} %copy-done.1, f32[4,128,256]{2,1,0:T(8,128)S(1)} %copy-done, f32[4,128,256]{2,1,0:T(8,128)S(1)} %get-tuple-element.4, f32[4,128,256]{2,1,0:T(8,128)S(1)} %get-tuple-element.17), kind=kLoop, calls=%fused_computation.42 | loop fusion | flops 1966080 | bytes 3145728 | tf_op jit(solution)/shard_map/div | solution.py:101
  137.8 15.5 %psum.31 = f32[3]{0:T(128)S(1)} all-reduce(f32[3]{0:T(128)S(1)} %psum.30), channel_id=1, replica_groups=mesh['tm'=4,'row'=16,'col_0'=4,'col_1'=2] {'col_1'}, use_global_device_ids=true, to_apply=%region_6.7 | all-reduce | flops 3 | bytes 24 | tf_op jit(solution)/shard_map/psum | solution.py:24
  (63 shorter events, 8.7 us)
Async XLA Ops:
  0.6 9.8 %copy-start = (f32[4,128,256]{2,1,0:T(8,128)S(1)}, f32[4,128,256]{2,1,0:T(8,128)}, u32[]{:S(2)}) copy-start(f32[4,128,256]{2,1,0:T(8,128)} %param.2) | copy-start | bytes 1572868
  1.7 11.7 %collective-permute-start.2 = (f32[4,128,1]{2,1,0:T(8,128)S(1)}, f32[4,128,1]{2,1,0:T(8,128)S(1)}, u32[]{:S(2)}, u32[]{:S(2)}) collective-permute-start(f32[4,128,1]{2,1,0:T(8,128)S(1)} %slice.143), channel_id=1, source_target_pairs={{1,0},{2,1},{3,2},{4,3},{5,4},{6,5},{7,6},{9,8},{10,9},{11,10},{12... | collective-permute-start | bytes 6152 | tf_op jit(solution)/shard_map/ppermute | solution.py:19
  10.5 4.5 %collective-permute-start.1 = (f32[4,1,256]{2,1,0:T(1,128)S(1)}, f32[4,1,256]{2,1,0:T(1,128)S(1)}, u32[]{:S(2)}, u32[]{:S(2)}) collective-permute-start(f32[4,1,256]{2,1,0:T(1,128)S(1)} %slice.140), channel_id=1, source_target_pairs={{8,0},{16,8},{24,16},{32,24},{40,32},{48,40},{56,48},{64,56},{72,6... | collective-permute-start | bytes 12296 | tf_op jit(solution)/shard_map/ppermute | solution.py:19
  11.8 7.1 %collective-permute-start = (f32[1,128,256]{2,1,0:T(8,128)S(1)}, f32[1,128,256]{2,1,0:T(8,128)S(1)}, u32[]{:S(2)}, u32[]{:S(2)}) collective-permute-start(f32[1,128,256]{2,1,0:T(8,128)S(1)} %slice.137), channel_id=1, source_target_pairs={{128,0},{256,128},{384,256},{129,1},{257,129},{385,257},{130,2},{2... | collective-permute-start | bytes 393224 | tf_op jit(solution)/shard_map/ppermute | solution.py:19
  19.4 11.0 %collective-permute-start.3 = (f32[1,128,256]{2,1,0:T(8,128)S(1)}, f32[1,128,256]{2,1,0:T(8,128)S(1)}, u32[]{:S(2)}, u32[]{:S(2)}) collective-permute-start(f32[1,128,256]{2,1,0:T(8,128)S(1)} %slice.180), channel_id=1, source_target_pairs={{0,128},{128,256},{256,384},{1,129},{129,257},{257,385},{2,130},{1... | collective-permute-start | bytes 393224 | tf_op jit(solution)/shard_map/ppermute | solution.py:19
  20.8 9.6 %collective-permute-start.4 = (f32[4,1,256]{2,1,0:T(1,128)S(1)}, f32[4,1,256]{2,1,0:T(1,128)S(1)}, u32[]{:S(2)}, u32[]{:S(2)}) collective-permute-start(f32[4,1,256]{2,1,0:T(1,128)S(1)} %slice.182), channel_id=1, source_target_pairs={{0,8},{8,16},{16,24},{24,32},{32,40},{40,48},{48,56},{56,64},{64,7... | collective-permute-start | bytes 12296 | tf_op jit(solution)/shard_map/ppermute | solution.py:19
  25.0 5.4 %copy-start.1 = (f32[4,128,256]{2,1,0:T(8,128)S(1)}, f32[4,128,256]{2,1,0:T(8,128)}, u32[]{:S(2)}) copy-start(f32[4,128,256]{2,1,0:T(8,128)} %param.3) | copy-start | bytes 1572868
  25.0 5.4 %collective-permute-start.5 = (f32[4,128,1]{2,1,0:T(8,128)S(1)}, f32[4,128,1]{2,1,0:T(8,128)S(1)}, u32[]{:S(2)}, u32[]{:S(2)}) collective-permute-start(f32[4,128,1]{2,1,0:T(8,128)S(1)} %slice.184), channel_id=1, source_target_pairs={{0,1},{1,2},{2,3},{3,4},{4,5},{5,6},{6,7},{8,9},{9,10},{10,11},{11... | collective-permute-start | bytes 6152 | tf_op jit(solution)/shard_map/ppermute | solution.py:19
  30.9 8.4 %collective-permute-start.8 = (f32[4,128,1]{2,1,0:T(8,128)S(1)}, f32[4,128,1]{2,1,0:T(8,128)S(1)}, u32[]{:S(2)}, u32[]{:S(2)}) collective-permute-start(f32[4,128,1]{2,1,0:T(8,128)S(1)} %slice.194), channel_id=1, source_target_pairs={{1,0},{2,1},{3,2},{4,3},{5,4},{6,5},{7,6},{9,8},{10,9},{11,10},{12... | collective-permute-start | bytes 6152 | tf_op jit(solution)/shard_map/ppermute | solution.py:19
  33.1 6.3 %collective-permute-start.7 = (f32[4,1,256]{2,1,0:T(1,128)S(1)}, f32[4,1,256]{2,1,0:T(1,128)S(1)}, u32[]{:S(2)}, u32[]{:S(2)}) collective-permute-start(f32[4,1,256]{2,1,0:T(1,128)S(1)} %slice.191), channel_id=1, source_target_pairs={{8,0},{16,8},{24,16},{32,24},{40,32},{48,40},{56,48},{64,56},{72,6... | collective-permute-start | bytes 12296 | tf_op jit(solution)/shard_map/ppermute | solution.py:19
  34.4 5.7 %collective-permute-start.6 = (f32[1,128,256]{2,1,0:T(8,128)S(1)}, f32[1,128,256]{2,1,0:T(8,128)S(1)}, u32[]{:S(2)}, u32[]{:S(2)}) collective-permute-start(f32[1,128,256]{2,1,0:T(8,128)S(1)} %slice.188), channel_id=1, source_target_pairs={{128,0},{256,128},{384,256},{129,1},{257,129},{385,257},{130,2},{2... | collective-permute-start | bytes 393224 | tf_op jit(solution)/shard_map/ppermute | solution.py:19
  40.9 16.8 %collective-permute-start.9 = (f32[1,128,256]{2,1,0:T(8,128)S(1)}, f32[1,128,256]{2,1,0:T(8,128)S(1)}, u32[]{:S(2)}, u32[]{:S(2)}) collective-permute-start(f32[1,128,256]{2,1,0:T(8,128)S(1)} %slice.195), channel_id=1, source_target_pairs={{0,128},{128,256},{256,384},{1,129},{129,257},{257,385},{2,130},{1... | collective-permute-start | bytes 393224 | tf_op jit(solution)/shard_map/ppermute | solution.py:19
  43.0 14.7 %collective-permute-start.10 = (f32[4,1,256]{2,1,0:T(1,128)S(1)}, f32[4,1,256]{2,1,0:T(1,128)S(1)}, u32[]{:S(2)}, u32[]{:S(2)}) collective-permute-start(f32[4,1,256]{2,1,0:T(1,128)S(1)} %slice.197), channel_id=1, source_target_pairs={{0,8},{8,16},{16,24},{24,32},{32,40},{40,48},{48,56},{56,64},{64,7... | collective-permute-start | bytes 12296 | tf_op jit(solution)/shard_map/ppermute | solution.py:19
  47.3 10.3 %collective-permute-start.11 = (f32[4,128,1]{2,1,0:T(8,128)S(1)}, f32[4,128,1]{2,1,0:T(8,128)S(1)}, u32[]{:S(2)}, u32[]{:S(2)}) collective-permute-start(f32[4,128,1]{2,1,0:T(8,128)S(1)} %slice.199), channel_id=1, source_target_pairs={{0,1},{1,2},{2,3},{3,4},{4,5},{5,6},{6,7},{8,9},{9,10},{10,11},{11... | collective-permute-start | bytes 6152 | tf_op jit(solution)/shard_map/ppermute | solution.py:19
  59.9 8.4 %collective-permute-start.14 = (f32[4,128,1]{2,1,0:T(8,128)S(1)}, f32[4,128,1]{2,1,0:T(8,128)S(1)}, u32[]{:S(2)}, u32[]{:S(2)}) collective-permute-start(f32[4,128,1]{2,1,0:T(8,128)S(1)} %slice.209), channel_id=1, source_target_pairs={{1,0},{2,1},{3,2},{4,3},{5,4},{6,5},{7,6},{9,8},{10,9},{11,10},{12... | collective-permute-start | bytes 6152 | tf_op jit(solution)/shard_map/ppermute | solution.py:19
  62.1 6.3 %collective-permute-start.13 = (f32[4,1,256]{2,1,0:T(1,128)S(1)}, f32[4,1,256]{2,1,0:T(1,128)S(1)}, u32[]{:S(2)}, u32[]{:S(2)}) collective-permute-start(f32[4,1,256]{2,1,0:T(1,128)S(1)} %slice.206), channel_id=1, source_target_pairs={{8,0},{16,8},{24,16},{32,24},{40,32},{48,40},{56,48},{64,56},{72,6... | collective-permute-start | bytes 12296 | tf_op jit(solution)/shard_map/ppermute | solution.py:19
  63.4 5.7 %collective-permute-start.12 = (f32[1,128,256]{2,1,0:T(8,128)S(1)}, f32[1,128,256]{2,1,0:T(8,128)S(1)}, u32[]{:S(2)}, u32[]{:S(2)}) collective-permute-start(f32[1,128,256]{2,1,0:T(8,128)S(1)} %slice.203), channel_id=1, source_target_pairs={{128,0},{256,128},{384,256},{129,1},{257,129},{385,257},{130,2},{2... | collective-permute-start | bytes 393224 | tf_op jit(solution)/shard_map/ppermute | solution.py:19
  70.0 16.3 %collective-permute-start.15 = (f32[1,128,256]{2,1,0:T(8,128)S(1)}, f32[1,128,256]{2,1,0:T(8,128)S(1)}, u32[]{:S(2)}, u32[]{:S(2)}) collective-permute-start(f32[1,128,256]{2,1,0:T(8,128)S(1)} %slice.210), channel_id=1, source_target_pairs={{0,128},{128,256},{256,384},{1,129},{129,257},{257,385},{2,130},{1... | collective-permute-start | bytes 393224 | tf_op jit(solution)/shard_map/ppermute | solution.py:19
  71.7 14.7 %collective-permute-start.16 = (f32[4,1,256]{2,1,0:T(1,128)S(1)}, f32[4,1,256]{2,1,0:T(1,128)S(1)}, u32[]{:S(2)}, u32[]{:S(2)}) collective-permute-start(f32[4,1,256]{2,1,0:T(1,128)S(1)} %slice.212), channel_id=1, source_target_pairs={{0,8},{8,16},{16,24},{24,32},{32,40},{40,48},{48,56},{56,64},{64,7... | collective-permute-start | bytes 12296 | tf_op jit(solution)/shard_map/ppermute | solution.py:19
  76.3 10.0 %collective-permute-start.17 = (f32[4,128,1]{2,1,0:T(8,128)S(1)}, f32[4,128,1]{2,1,0:T(8,128)S(1)}, u32[]{:S(2)}, u32[]{:S(2)}) collective-permute-start(f32[4,128,1]{2,1,0:T(8,128)S(1)} %slice.214), channel_id=1, source_target_pairs={{0,1},{1,2},{2,3},{3,4},{4,5},{5,6},{6,7},{8,9},{9,10},{10,11},{11... | collective-permute-start | bytes 6152 | tf_op jit(solution)/shard_map/ppermute | solution.py:19
where the time goes:
time: 154 us
  blocking collectives  60 us (39%)
  starting transfers between devices  54 us (35%)
  waiting for transfers between devices  23.6 us (15%)
  other arithmetic  12.5 us (8%)
  local copies, waits for them, and re-layouts  2.43 us (2%)
    psum x4, blocking collectives, one_axis_at_a_time(): value = lax.psum(value, axis)  60 us
    ppermute x18, starting transfers between devices, shifted(): return lax.ppermute(block, axis, route)  54 us
    ppermute x18, waiting for transfers between devices, shifted(): return lax.ppermute(block, axis, route)  23.6 us
    reduce_sum x2, other arithmetic, on_device(): local_sum = jnp.sum(term)  4.73 us
  transfers between devices with their start and end apart: 18, of which 9 were waited for; matrix products, arithmetic and copies ran while one was open for 1% of the time, Pallas kernels for 0%

commit v1 on v0

v1 whole, which is shorter than its diff:
```python
import functools

import jax
import jax.numpy as jnp
from jax import lax
from jax.experimental import pallas as pl
from jax.experimental.pallas import tpu as pltpu
from jax.sharding import PartitionSpec as P

SIG = 0.28
TAU = 0.28

FR = 4
NT = 16
NTE = 17
NF = 10
NL = 8
LW = 3
LOFF = 64


def iota(axis):
    return lax.broadcasted_iota(jnp.int32, (8, 128), axis)


def tile(ref, lead, i, j):
    return ref[lead, i * 8 : (i + 1) * 8, j * 128 : (j + 1) * 128]


def put(ref, lead, i, j, value):
    ref[lead, i * 8 : (i + 1) * 8, j * 128 : (j + 1) * 128] = value


def lanes_of(lane, planes):
    hit = None
    for p in planes:
        for base in (0, LOFF):
            here = (lane >= base + LW * p) & (lane < base + LW * p + LW)
            hit = here if hit is None else hit | here
    return hit


def pack_kernel(f_ref, l_ref, s_ref, up_ref, dn_ref):
    sub, lane = iota(0), iota(1)
    for i in range(NT):
        acc = jnp.zeros((8, 128), jnp.float32)
        for t in range(FR):
            for ref, p in ((f_ref, t + 3), (l_ref, t + 12)):
                right = pltpu.roll(tile(ref, t, i, 1), (LW * p - 125) % 128, 1)
                left = pltpu.roll(tile(ref, t, i, 0), (LOFF + LW * p) % 128, 1)
                acc = jnp.where((lane >= LW * p) & (lane < LW * p + LW), right, acc)
                acc = jnp.where((lane >= LOFF + LW * p) & (lane < LOFF + LW * p + LW), left, acc)
        s_ref[i] = acc
    for t in range(FR):
        for k, ref in ((0, f_ref), (4, l_ref)):
            for j in range(2):
                s_ref[NT + 2 * (t + k) + j] = jnp.where(sub < 4, tile(ref, t, 0, j), tile(ref, t, NT - 1, j))
    up_ref[0:3] = f_ref[1:4]
    up_ref[3:5] = l_ref[2:4]
    dn_ref[0:3] = f_ref[0:3]
    dn_ref[3:5] = l_ref[0:2]


def rows_kernel(own_ref, prev_ref, next_ref, z_ref):
    def move(src, plane, dst):
        for j in range(2):
            z_ref[2 * dst + j] = src[NT + 2 * plane + j]

    for k in range(3):
        move(prev_ref, k + 1, k)
        move(next_ref, k, 7 + k)
    for k in range(4):
        move(own_ref, k, 3 + k)
        move(own_ref, 4 + k, 12 + k)
    for k in range(2):
        move(prev_ref, 6 + k, 10 + k)
        move(next_ref, 4 + k, 16 + k)


def cols_kernel(own_ref, prev_ref, next_ref, zp_ref, zn_ref, m_ref):
    sub, lane = iota(0), iota(1)
    from_prev = lanes_of(lane, (0, 1, 2, 10, 11))
    from_next = lanes_of(lane, (7, 8, 9, 16, 17))
    for i in range(NT):
        a = pltpu.roll(prev_ref[i], 128 - 12, 1)
        b = pltpu.roll(next_ref[i], 12, 1)
        m_ref[i] = jnp.where(from_prev, a, jnp.where(from_next, b, own_ref[i]))
    acc = jnp.zeros((8, 128), jnp.float32)
    for p in range(NF + NL):
        left = jnp.where(sub < 4, zn_ref[2 * p], zp_ref[2 * p])
        right = jnp.where(sub < 4, zn_ref[2 * p + 1], zp_ref[2 * p + 1])
        right = pltpu.roll(right, (LW * p - 125) % 128, 1)
        left = pltpu.roll(left, (LOFF + LW * p) % 128, 1)
        acc = jnp.where((lane >= LW * p) & (lane < LW * p + LW), right, acc)
        acc = jnp.where((lane >= LOFF + LW * p) & (lane < LOFF + LW * p + LW), left, acc)
    m_ref[NT] = acc


def main_kernel(
    sizes, f_ref, l_ref, bp_ref, bn_ref, zp_ref, zn_ref, mp_ref, mn_ref,
    out_ref, sum_ref,
    ua, ub, qa, qb, v1, v2, wt, at, il, g1, g2,
):
    n_tm, n_row, n_col = sizes
    sub, lane = iota(0), iota(1)
    first_t = lax.axis_index("tm") == 0
    last_t = lax.axis_index("tm") == n_tm - 1
    one, zero = jnp.float32(1.0), jnp.float32(0.0)
    last_r = jnp.where(lax.axis_index("row") == n_row - 1, zero, one)
    first_r = jnp.where(lax.axis_index("row") == 0, zero, one)
    last_c = jnp.where(lax.axis_index("col") == n_col - 1, zero, one)
    first_c = jnp.where(lax.axis_index("col") == 0, zero, one)
    ones = jnp.ones((8, 128), jnp.float32)
    row_mask = {NT - 1: jnp.where(sub == 7, ones * last_r, ones), NT: jnp.where(sub == 7, ones * first_r, ones)}
    col_mask = {1: jnp.where(lane == 127, ones * last_c, ones), 2: jnp.where(lane == 127, ones * first_c, ones)}

    def prim(lam, noisy):
        scaled = TAU * lam
        return 1.0 / (1.0 + scaled), scaled * noisy

    def fill_noisy(src, at0, dst):
        for i in range(NT):
            for j in range(2):
                put(ua, dst, i, j, tile(src, at0, i, j))

    def fill_lam(src, at0, dst):
        for i in range(NT):
            for j in range(2):
                w, a = prim(tile(src, at0, i, j), tile(ua, dst + 1, i, j))
                put(wt, dst, i, j, w)
                put(at, dst, i, j, a)

    def own(t, c):
        fill_noisy(f_ref, t, t + 3)
        for i in range(NT):
            for j in range(2):
                lam = tile(l_ref, t, i, j)
                w, a = prim(lam, tile(f_ref, t, i, j))
                put(wt, t + 2, i, j, w)
                put(at, t + 2, i, j, a)
                put(il, t, i, j, 0.5 / lam)
        return c

    lax.fori_loop(0, FR, own, 0)

    def face(k, c):
        fill_noisy(bp_ref, k, k)
        fill_noisy(bn_ref, k, k + 7)
        return c

    lax.fori_loop(0, 3, face, 0)

    def face_lam(k, c):
        fill_lam(bp_ref, 3 + k, k)
        fill_lam(bn_ref, 3 + k, 6 + k)
        return c

    lax.fori_loop(0, 2, face_lam, 0)
    for p in range(NF + NL):
        for j in range(2):
            z = jnp.where(sub < 4, zn_ref[2 * p + j], zp_ref[2 * p + j])
            if p < NF:
                put(ua, p, NT, j, z)
            else:
                w, a = prim(z, tile(ua, p - NF + 1, NT, j))
                put(wt, p - NF, NT, j, w)
                put(at, p - NF, NT, j, a)

    def side(i, c):
        rows = pl.ds(pl.multiple_of(i * 8, 8), 8)
        mp, mn = mp_ref[i], mn_ref[i]
        noisy = []
        for p in range(NF + NL):
            right = pltpu.roll(mn, (-(LOFF + LW * p)) % 128, 1)
            left = pltpu.roll(mp, (125 - LW * p) % 128, 1)
            x = jnp.where(lane < 3, right, jnp.where(lane >= 125, left, 0.0))
            if p < NF:
                ua[p, rows, 256:384] = x
                noisy.append(x)
            else:
                w, a = prim(x, noisy[p - NF + 1])
                wt[p - NF, rows, 256:384] = w
                at[p - NF, rows, 256:384] = a
        return c

    lax.fori_loop(0, NTE, side, 0)

    def dual_step(step, u, qi, qo, tt, gi, go, acc):
        inside = acc is not None
        keep = jnp.where(((tt == 6) & last_t) | ((tt == 2) & first_t), zero, one)
        here = [tile(u, tt, 0, j) for j in range(3)]
        start = here
        for i in range(NTE):
            after = start if i == NT else [tile(u, tt, i + 1, j) for j in range(3)]
            turned = [pltpu.roll(here[j], 127, 1) for j in range(3)]
            for j in range(3):
                x = here[j]
                d0 = (tile(u, tt + 1, i, j) - x) * keep
                d1 = pltpu.roll(jnp.where(sub == 0, after[j], x), 7, 0) - x
                if i in row_mask:
                    d1 = d1 * row_mask[i]
                d2 = jnp.where(lane == 127, turned[(j + 1) % 3], turned[j]) - x
                if j in col_mask:
                    d2 = d2 * col_mask[j]
                d = (d0, d1, d2)
                if inside and i < NT and j < 2:
                    gu = d
                    t = tt - 3
                    if step > 0:
                        gu = tuple(0.5 * (d[k] + tile(gi, 4 * k + t, i, j)) for k in range(3))
                    if step < 2:
                        for k in range(3):
                            put(go, 4 * k + t, i, j, gu[k])
                    acc[j] = acc[j] + jnp.sqrt(gu[0] * gu[0] + gu[1] * gu[1] + gu[2] * gu[2])
                m = d if step == 0 else tuple(d[k] + tile(qi, NF * k + tt, i, j) for k in range(3))
                n2 = (m[0] * m[0] + m[1] * m[1] + m[2] * m[2]) * (SIG * SIG)
                s = jnp.minimum(1.0, lax.rsqrt(n2))
                for k in range(3):
                    put(qo, NF * k + tt, i, j, m[k] * s)
            here = after

    def primal_step(step, u, q, vi, vo, uo, tt, acc):
        inside = acc is not None
        nj = 3 if step < 2 else 2
        before = [tile(q, NF + tt, NT, j) for j in range(nj)]
        for i in range(NTE if step < 2 else NT):
            rows = [tile(q, NF + tt, i, j) for j in range(nj)]
            cols = [tile(q, 2 * NF + tt, i, j) for j in range(3)]
            turned = [pltpu.roll(cols[j], 1, 1) for j in range(3)]
            for j in range(nj):
                d = tile(q, tt, i, j) - tile(q, tt - 1, i, j)
                d = d + (rows[j] - pltpu.roll(jnp.where(sub == 7, before[j], rows[j]), 1, 0))
                d = d + (cols[j] - jnp.where(lane == 0, turned[j - 1], turned[j]))
                old = tile(u, tt, i, j) if step == 0 else tile(vi, tt, i, j)
                new = (old + (TAU * SIG) * d + tile(at, tt - 1, i, j)) * tile(wt, tt - 1, i, j)
                if step < 2:
                    put(vo, tt, i, j, new)
                    put(uo, tt, i, j, 2.0 * new - old)
                else:
                    put(out_ref, tt - 3, i, j, new)
                if inside and i < NT and j < 2:
                    t = tt - 3
                    e = SIG * d
                    noisy = tile(f_ref, t, i, j)
                    term = e * (e * tile(il, t, i, j) + noisy)
                    if step > 0:
                        r = old - noisy
                        term = term + (0.5 * tile(l_ref, t, i, j)) * (r * r)
                    acc[j] = acc[j] + term
            before = rows

    def run(step, u, uo, qi, qo, vi, vo, gi, go):
        lo, hi = step, 8 - step

        def dual_out(k, c):
            dual_step(step, u, qi, qo, jnp.where(k < 3, k, k + 4), gi, go, None)
            return c

        def dual_in(tt, c):
            acc = list(c)
            dual_step(step, u, qi, qo, tt, gi, go, acc)
            return tuple(acc)

        def primal_out(k, c):
            primal_step(step, u, qo, vi, vo, uo, jnp.where(k < 3, k, k + 4), None)
            return c

        def primal_in(tt, c):
            acc = list(c)
            primal_step(step, u, qo, vi, vo, uo, tt, acc)
            return tuple(acc)

        blank = jnp.zeros((8, 128), jnp.float32)
        lax.fori_loop(lo, hi - 3, dual_out, 0)
        acc = lax.fori_loop(3, 7, dual_in, (blank, blank))
        if step < 2:
            lax.fori_loop(lo + 1, hi - 3, primal_out, 0)
        acc = lax.fori_loop(3, 7, primal_in, acc)
        return acc[0] + acc[1]

    s0 = run(0, ua, ub, qb, qa, None, v1, None, g1)
    s1 = run(1, ub, ua, qa, qb, v1, v2, g1, g2)
    s2 = run(2, ua, None, qb, qa, v2, None, g2, None)
    total = [jnp.sum(s) for s in (s0, s1, s2)]
    col = lax.broadcasted_iota(jnp.int32, sum_ref.shape, 1)
    sum_ref[...] = jnp.where(col == 0, total[0], jnp.where(col == 1, total[1], jnp.where(col == 2, total[2], 0.0)))


VMEM = pl.BlockSpec(memory_space=pltpu.VMEM)


def call(kernel, outs, *args, flops, scratch=(), limit=None):
    return pl.pallas_call(
        kernel,
        out_shape=outs,
        in_specs=[VMEM] * len(args),
        out_specs=jax.tree.map(lambda _: VMEM, outs),
        scratch_shapes=scratch,
        cost_estimate=pl.CostEstimate(flops=flops, bytes_accessed=1 << 20, transcendentals=0),
        compiler_params=pltpu.CompilerParams(vmem_limit_bytes=limit),
    )(*args)


def f32(*shape):
    return jax.ShapeDtypeStruct(shape, jnp.float32)


def both_ways(later, earlier, axis):
    n = lax.axis_size(axis)
    onward = lax.ppermute(later, axis, [(i, i + 1) for i in range(n - 1)])
    back = lax.ppermute(earlier, axis, [(i + 1, i) for i in range(n - 1)])
    return onward, back


def on_device(noisy, lam):
    n_tm, n_row, n_col = (lax.axis_size(a) for a in ("tm", "row", "col"))
    cells = float(noisy.size * n_tm * n_row * n_col)
    strip, up, down = call(
        pack_kernel, (f32(NT + 16, 8, 128), f32(5, 128, 256), f32(5, 128, 256)), noisy, lam, flops=1 << 20
    )
    sp, sn = both_ways(strip, strip, "tm")
    up, down, _, _ = lax.optimization_barrier((up, down, strip, strip))
    bp, bn = both_ways(up, down, "tm")
    z = call(rows_kernel, f32(2 * (NF + NL), 8, 128), strip, sp, sn, flops=1 << 20)
    zp, zn = both_ways(z, z, "row")
    m = call(cols_kernel, f32(NTE, 8, 128), strip, sp, sn, zp, zn, flops=1 << 20)
    mp, mn = both_ways(m, m, "col")
    ext = lambda n: pltpu.VMEM((n, NTE * 8, 384), jnp.float32)
    inner = lambda n: pltpu.VMEM((n, 128, 256), jnp.float32)
    out, rows = call(
        functools.partial(main_kernel, (n_tm, n_row, n_col)),
        (f32(4, 128, 256), f32(n_row, 128)),
        noisy, lam, bp, bn, zp, zn, mp, mn,
        flops=1 << 26,
        scratch=[ext(NF), ext(NF), ext(3 * NF), ext(3 * NF), ext(NF), ext(NF), ext(NL), ext(NL), inner(4), inner(12), inner(12)],
        limit=40 << 20,
    )
    part = jnp.sum(lax.all_to_all(rows, "row", 0, 0, tiled=True), 0, keepdims=True)
    part = jnp.broadcast_to(part, (n_tm * n_col, 128))
    part = jnp.sum(lax.all_to_all(part, ("tm", "col"), 0, 0, tiled=True), 0)
    gaps = part[:3] / cells
    return out, gaps


def solution(mesh):
    spec = P("tm", "row", "col")
    return jax.shard_map(on_device, mesh=mesh, in_specs=(spec, spec), out_specs=(spec, P()), check_vma=False)
```

time: 154 us -> 108 us (0.70)
  starting transfers between devices: 54 us -> 26.7 us
  blocking collectives: 60 us -> 39.9 us
  Pallas kernels: 0 us -> 17.1 us
  other arithmetic: 12.5 us -> 0.57 us
  waiting for transfers between devices: 23.6 us -> 19.4 us
    psum x4 -> x0, blocking collectives: 60 us -> none  [one_axis_at_a_time(): value = lax.psum(value, axis)]
    all_to_all x0 -> x2, blocking collectives: none -> 39.9 us  [the longest x1 25.9 us: on_device(): lax.all_to_all(rows, 'row', 0, 0, tiled=True)]
    ppermute x18 -> x8, starting transfers between devices: 54 us -> 26.7 us  [the longest x4 20.9 us: both_ways(): onward = lax.ppermute(later, axis, [(i, i + 1) for i in range(n - 1)])]
    pallas_call x0 -> x4, Pallas kernels: none -> 17.1 us  [call(): pl.pallas_call(kernel, out_shape=outs, in_specs=[VMEM] * len(args), out_s...]
    reduce_sum x2, other arithmetic: 4.73 us -> 0.05 us  [the longest x1 0.03 us: on_device(): jnp.sum(lax.all_to_all(rows, 'row', 0, 0, tiled=True), 0, keepdims=True)]
    ppermute x18 -> x8, waiting for transfers between devices: 23.6 us -> 19.4 us  [the longest x4 11.5 us: both_ways(): back = lax.ppermute(earlier, axis, [(i + 1, i) for i in range(n - 1)])]
    div x7 -> x1, other arithmetic: 4.62 us -> 0.52 us  [on_device(): gaps = part[:3] / cells]
    unnamed x4 -> x16, local copies, waits for them, and re-layouts: 0.01 us -> 3.14 us
  transfers between devices with their start and end apart: 18 -> 8, of which waited for: 9 -> 5; matrix products, arithmetic and copies ran while one was open for 1% -> 0% of each run, Pallas kernels for 0% -> 3%
where the time goes in v1:
time: 108 us; the launch traced here: 107 us
  blocking collectives  39.9 us (37%)
  starting transfers between devices  26.7 us (25%)
  waiting for transfers between devices  19.4 us (18%)
  Pallas kernels  17.1 us (16%)
  local copies, waits for them, and re-layouts  3.15 us (3%)
    all_to_all x1, blocking collectives, on_device(): lax.all_to_all(rows, 'row', 0, 0, tiled=True)  25.9 us
    ppermute x4, starting transfers between devices, both_ways(): onward = lax.ppermute(later, axis, [(i, i + 1) for i in range(n - 1)])  20.9 us
    pallas_call x4, Pallas kernels, call(): pl.pallas_call(kernel, out_shape=outs, in_specs=[VMEM] * len(args), out_s...  17.1 us
    all_to_all x1, blocking collectives, on_device(): part = jnp.sum(lax.all_to_all(part, ('tm', 'col'), 0, 0, tiled=True), 0)  14 us
    ppermute x4, waiting for transfers between devices, both_ways(): back = lax.ppermute(earlier, axis, [(i + 1, i) for i in range(n - 1)])  11.5 us
    ppermute x4, waiting for transfers between devices, both_ways(): onward = lax.ppermute(later, axis, [(i, i + 1) for i in range(n - 1)])  7.82 us
    ppermute x4, starting transfers between devices, both_ways(): back = lax.ppermute(earlier, axis, [(i + 1, i) for i in range(n - 1)])  5.8 us
    unnamed x16, local copies, waits for them, and re-layouts  3.14 us
  transfers between devices with their start and end apart: 8, of which 5 were waited for; matrix products, arithmetic and copies ran while one was open for 0% of the time, Pallas kernels for 3%

profile of v1, /device:TPU:1, one launch (start us, length us, event | category | flops | bytes accessed | tf_op | source)
XLA Modules:
  0.0 107.5 jit_solution(2421756851316294825)
XLA Ops:
  0.6 2.6 %shard_map.41 = (f32[32,8,128]{2,1,0:T(8,128)}, f32[5,128,256]{2,1,0:T(8,128)}, f32[5,128,256]{2,1,0:T(8,128)}) custom-call(f32[4,128,256]{2,1,0:T(8,128)} %f_ref.3, f32[4,128,256]{2,1,0:T(8,128)} %l_ref.3), custom_call_target="tpu_custom_call" | custom-call | flops 1048576 | bytes 1048576 | tf_op jit(solution)/shard_map/pallas_call | solution.py:293
  3.2 4.2 %collective-permute-start = (f32[5,128,256]{2,1,0:T(8,128)}, f32[5,128,256]{2,1,0:T(8,128)S(1)}, u32[]{:S(2)}, u32[]{:S(2)}) collective-permute-start(f32[5,128,256]{2,1,0:T(8,128)} %get-tuple-element.12), channel_id=1, source_target_pairs={{0,128},{128,256},{256,384},{1,129},{129,257},{257,385},{2,130},{1... | collective-permute-start | bytes 1966088 | tf_op jit(solution)/shard_map/ppermute | solution.py:310
  7.4 1.3 %collective-permute-start.1 = (f32[5,128,256]{2,1,0:T(8,128)}, f32[5,128,256]{2,1,0:T(8,128)S(1)}, u32[]{:S(2)}, u32[]{:S(2)}) collective-permute-start(f32[5,128,256]{2,1,0:T(8,128)} %get-tuple-element.13), channel_id=1, source_target_pairs={{128,0},{256,128},{384,256},{129,1},{257,129},{385,257},{130,2},{2... | collective-permute-start | bytes 1966088 | tf_op jit(solution)/shard_map/ppermute | solution.py:311
  8.7 4.0 %collective-permute-start.2 = (f32[32,8,128]{2,1,0:T(8,128)}, f32[32,8,128]{2,1,0:T(8,128)S(1)}, u32[]{:S(2)}, u32[]{:S(2)}) collective-permute-start(f32[32,8,128]{2,1,0:T(8,128)} %get-tuple-element.11.own_ref), channel_id=1, source_target_pairs={{0,128},{128,256},{256,384},{1,129},{129,257},{257,385},{2,130},{1... | collective-permute-start | bytes 393224 | tf_op jit(solution)/shard_map/ppermute | solution.py:310
  12.7 1.3 %collective-permute-start.3 = (f32[32,8,128]{2,1,0:T(8,128)}, f32[32,8,128]{2,1,0:T(8,128)S(1)}, u32[]{:S(2)}, u32[]{:S(2)}) collective-permute-start(f32[32,8,128]{2,1,0:T(8,128)} %get-tuple-element.11.own_ref), channel_id=1, source_target_pairs={{128,0},{256,128},{384,256},{129,1},{257,129},{385,257},{130,2},{2... | collective-permute-start | bytes 393224 | tf_op jit(solution)/shard_map/ppermute | solution.py:311
  14.0 6.7 %collective-permute-done.2.prev_ref = f32[32,8,128]{2,1,0:T(8,128)S(1)} collective-permute-done((f32[32,8,128]{2,1,0:T(8,128)}, f32[32,8,128]{2,1,0:T(8,128)S(1)}, u32[]{:S(2)}, u32[]{:S(2)}) %collective-permute-start.2) | collective-permute-done | bytes 131104 | tf_op jit(solution)/shard_map/ppermute | solution.py:310
  20.8 3.8 %collective-permute-done.3.next_ref = f32[32,8,128]{2,1,0:T(8,128)S(1)} collective-permute-done((f32[32,8,128]{2,1,0:T(8,128)}, f32[32,8,128]{2,1,0:T(8,128)S(1)}, u32[]{:S(2)}, u32[]{:S(2)}) %collective-permute-start.3) | collective-permute-done | bytes 131104 | tf_op jit(solution)/shard_map/ppermute | solution.py:311
  24.5 0.0 copy-done.6
  24.5 0.7 copy-done.7
  25.2 1.7 %shard_map.42 = f32[36,8,128]{2,1,0:T(8,128)} custom-call(f32[32,8,128]{2,1,0:T(8,128)} %get-tuple-element.11.own_ref, f32[32,8,128]{2,1,0:T(8,128)} %copy-done.6, f32[32,8,128]{2,1,0:T(8,128)} %copy-done.7), custom_call_target="tpu_custom_call" | custom-call | flops 1048576 | bytes 1048576 | tf_op jit(solution)/shard_map/pallas_call | solution.py:293
  26.9 6.7 %collective-permute-start.4 = (f32[36,8,128]{2,1,0:T(8,128)}, f32[36,8,128]{2,1,0:T(8,128)S(1)}, u32[]{:S(2)}, u32[]{:S(2)}) collective-permute-start(f32[36,8,128]{2,1,0:T(8,128)} %shard_map.42), channel_id=1, source_target_pairs={{0,8},{8,16},{16,24},{24,32},{32,40},{40,48},{48,56},{56,64},{64,7... | collective-permute-start | bytes 442376 | tf_op jit(solution)/shard_map/ppermute | solution.py:310
  33.6 1.3 %collective-permute-start.5 = (f32[36,8,128]{2,1,0:T(8,128)}, f32[36,8,128]{2,1,0:T(8,128)S(1)}, u32[]{:S(2)}, u32[]{:S(2)}) collective-permute-start(f32[36,8,128]{2,1,0:T(8,128)} %shard_map.42), channel_id=1, source_target_pairs={{8,0},{16,8},{24,16},{32,24},{40,32},{48,40},{56,48},{64,56},{72,6... | collective-permute-start | bytes 442376 | tf_op jit(solution)/shard_map/ppermute | solution.py:311
  34.9 1.1 %collective-permute-done.4.zp_ref = f32[36,8,128]{2,1,0:T(8,128)S(1)} collective-permute-done((f32[36,8,128]{2,1,0:T(8,128)}, f32[36,8,128]{2,1,0:T(8,128)S(1)}, u32[]{:S(2)}, u32[]{:S(2)}) %collective-permute-start.4) | collective-permute-done | bytes 147488 | tf_op jit(solution)/shard_map/ppermute | solution.py:310
  36.0 3.9 %collective-permute-done.5.zn_ref = f32[36,8,128]{2,1,0:T(8,128)S(1)} collective-permute-done((f32[36,8,128]{2,1,0:T(8,128)}, f32[36,8,128]{2,1,0:T(8,128)S(1)}, u32[]{:S(2)}, u32[]{:S(2)}) %collective-permute-start.5) | collective-permute-done | bytes 147488 | tf_op jit(solution)/shard_map/ppermute | solution.py:311
  39.9 0.0 copy-done.2
  39.9 0.7 copy-done.4
  40.5 1.9 %shard_map.43 = f32[17,8,128]{2,1,0:T(8,128)} custom-call(f32[32,8,128]{2,1,0:T(8,128)} %get-tuple-element.11.own_ref, f32[32,8,128]{2,1,0:T(8,128)} %copy-done.6, f32[32,8,128]{2,1,0:T(8,128)} %copy-done.7, f32[36,8,128]{2,1,0:T(8,128)} %copy-done.2, f32[36,8,128]{2,1,0:T(8,128)} %copy-done.4), custom_call_target="tpu_custom_call" | custom-call | flops 1048576 | bytes 1048576 | tf_op jit(solution)/shard_map/pallas_call | solution.py:293
  42.5 6.1 %collective-permute-start.6 = (f32[17,8,128]{2,1,0:T(8,128)}, f32[17,8,128]{2,1,0:T(8,128)S(1)}, u32[]{:S(2)}, u32[]{:S(2)}) collective-permute-start(f32[17,8,128]{2,1,0:T(8,128)} %shard_map.43), channel_id=1, source_target_pairs={{0,1},{1,2},{2,3},{3,4},{4,5},{5,6},{6,7},{8,9},{9,10},{10,11},{11... | collective-permute-start | bytes 208904 | tf_op jit(solution)/shard_map/ppermute | solution.py:310
  48.5 1.9 %collective-permute-start.7 = (f32[17,8,128]{2,1,0:T(8,128)}, f32[17,8,128]{2,1,0:T(8,128)S(1)}, u32[]{:S(2)}, u32[]{:S(2)}) collective-permute-start(f32[17,8,128]{2,1,0:T(8,128)} %shard_map.43), channel_id=1, source_target_pairs={{1,0},{2,1},{3,2},{4,3},{5,4},{6,5},{7,6},{9,8},{10,9},{11,10},{12... | collective-permute-start | bytes 208904 | tf_op jit(solution)/shard_map/ppermute | solution.py:311
  50.5 0.0 collective-permute-done.6.mp_ref
  50.5 3.9 %collective-permute-done.7.mn_ref = f32[17,8,128]{2,1,0:T(8,128)S(1)} collective-permute-done((f32[17,8,128]{2,1,0:T(8,128)}, f32[17,8,128]{2,1,0:T(8,128)S(1)}, u32[]{:S(2)}, u32[]{:S(2)}) %collective-permute-start.7) | collective-permute-done | bytes 69664 | tf_op jit(solution)/shard_map/ppermute | solution.py:311
  54.4 0.0 collective-permute-done.bp_ref
  54.4 0.0 collective-permute-done.1.bn_ref
  54.4 0.0 copy-done
  54.4 0.0 copy-done.1
  54.4 0.0 copy-start.3
  54.4 0.9 copy-done.3
  55.3 0.9 copy-done.5
  56.2 10.8 %shard_map.44 = (f32[4,128,256]{2,1,0:T(8,128)}, f32[16,128]{1,0:T(8,128)S(1)}) custom-call(f32[4,128,256]{2,1,0:T(8,128)S(1)} %copy-done, f32[4,128,256]{2,1,0:T(8,128)S(1)} %copy-done.1, f32[5,128,256]{2,1,0:T(8,128)S(1)} %collective-permute-done.bp_ref, f32[5,128,256]{2,1,0:T(8,128)S(1)} %collective-permute-done.1.bn_ref, f32[36,8,128]{2,1,0:T(8,128)S(1)} %copy-done.3, ...), custom_call_target="tpu_custom_call" | custom-call | flops 67108864 | bytes 1048576 | tf_op jit(solution)/shard_map/pallas_call | solution.py:293
  67.0 25.9 %all_to_all.15 = f32[16,1,128]{2,1,0:T(1,128)S(1)} all-to-all(f32[16,1,128]{2,1,0:T(1,128)S(1)} %bitcast.4), channel_id=1, replica_groups=mesh['tm'=4,'row'=16,'col'=8] {'row'}, dimensions={0} | all-to-all | bytes 16384 | tf_op jit(solution)/shard_map/all_to_all | solution.py:338
  93.0 14.0 %all_to_all.16 = f32[32,1,128]{2,1,0:T(1,128)S(1)} all-to-all(f32[32,1,128]{2,1,0:T(1,128)S(1)} %broadcast_in_dim.2), channel_id=1, replica_groups=mesh['tm'=4,'row'=16,'col'=8] {'tm','col'}, dimensions={0} | all-to-all | bytes 32768 | tf_op jit(solution)/shard_map/all_to_all | solution.py:340
  107.0 0.5 slice_multiply_fusion
  (10 shorter events, 0.1 us)
Async XLA Ops:
  3.2 51.1 %copy-start = (f32[4,128,256]{2,1,0:T(8,128)S(1)}, f32[4,128,256]{2,1,0:T(8,128)}, u32[]{:S(2)}) copy-start(f32[4,128,256]{2,1,0:T(8,128)} %f_ref.3) | copy-start | bytes 1572868
  3.2 51.1 %copy-start.1 = (f32[4,128,256]{2,1,0:T(8,128)S(1)}, f32[4,128,256]{2,1,0:T(8,128)}, u32[]{:S(2)}) copy-start(f32[4,128,256]{2,1,0:T(8,128)} %l_ref.3) | copy-start | bytes 1572868
  3.2 51.1 %collective-permute-start = (f32[5,128,256]{2,1,0:T(8,128)}, f32[5,128,256]{2,1,0:T(8,128)S(1)}, u32[]{:S(2)}, u32[]{:S(2)}) collective-permute-start(f32[5,128,256]{2,1,0:T(8,128)} %get-tuple-element.12), channel_id=1, source_target_pairs={{0,128},{128,256},{256,384},{1,129},{129,257},{257,385},{2,130},{1... | collective-permute-start | bytes 1966088 | tf_op jit(solution)/shard_map/ppermute | solution.py:310
  7.4 46.9 %collective-permute-start.1 = (f32[5,128,256]{2,1,0:T(8,128)}, f32[5,128,256]{2,1,0:T(8,128)S(1)}, u32[]{:S(2)}, u32[]{:S(2)}) collective-permute-start(f32[5,128,256]{2,1,0:T(8,128)} %get-tuple-element.13), channel_id=1, source_target_pairs={{128,0},{256,128},{384,256},{129,1},{257,129},{385,257},{130,2},{2... | collective-permute-start | bytes 1966088 | tf_op jit(solution)/shard_map/ppermute | solution.py:311
  8.7 12.0 %collective-permute-start.2 = (f32[32,8,128]{2,1,0:T(8,128)}, f32[32,8,128]{2,1,0:T(8,128)S(1)}, u32[]{:S(2)}, u32[]{:S(2)}) collective-permute-start(f32[32,8,128]{2,1,0:T(8,128)} %get-tuple-element.11.own_ref), channel_id=1, source_target_pairs={{0,128},{128,256},{256,384},{1,129},{129,257},{257,385},{2,130},{1... | collective-permute-start | bytes 393224 | tf_op jit(solution)/shard_map/ppermute | solution.py:310
  12.7 11.8 %collective-permute-start.3 = (f32[32,8,128]{2,1,0:T(8,128)}, f32[32,8,128]{2,1,0:T(8,128)S(1)}, u32[]{:S(2)}, u32[]{:S(2)}) collective-permute-start(f32[32,8,128]{2,1,0:T(8,128)} %get-tuple-element.11.own_ref), channel_id=1, source_target_pairs={{128,0},{256,128},{384,256},{129,1},{257,129},{385,257},{130,2},{2... | collective-permute-start | bytes 393224 | tf_op jit(solution)/shard_map/ppermute | solution.py:311
  20.8 3.8 %copy-start.6 = (f32[32,8,128]{2,1,0:T(8,128)}, f32[32,8,128]{2,1,0:T(8,128)S(1)}, u32[]{:S(2)}) copy-start(f32[32,8,128]{2,1,0:T(8,128)S(1)} %collective-permute-done.2.prev_ref) | copy-start | bytes 393220
  24.5 0.7 copy-start.7
  26.9 9.1 %collective-permute-start.4 = (f32[36,8,128]{2,1,0:T(8,128)}, f32[36,8,128]{2,1,0:T(8,128)S(1)}, u32[]{:S(2)}, u32[]{:S(2)}) collective-permute-start(f32[36,8,128]{2,1,0:T(8,128)} %shard_map.42), channel_id=1, source_target_pairs={{0,8},{8,16},{16,24},{24,32},{32,40},{40,48},{48,56},{56,64},{64,7... | collective-permute-start | bytes 442376 | tf_op jit(solution)/shard_map/ppermute | solution.py:310
  33.6 6.3 %collective-permute-start.5 = (f32[36,8,128]{2,1,0:T(8,128)}, f32[36,8,128]{2,1,0:T(8,128)S(1)}, u32[]{:S(2)}, u32[]{:S(2)}) collective-permute-start(f32[36,8,128]{2,1,0:T(8,128)} %shard_map.42), channel_id=1, source_target_pairs={{8,0},{16,8},{24,16},{32,24},{40,32},{48,40},{56,48},{64,56},{72,6... | collective-permute-start | bytes 442376 | tf_op jit(solution)/shard_map/ppermute | solution.py:311
  36.0 3.9 %copy-start.2 = (f32[36,8,128]{2,1,0:T(8,128)}, f32[36,8,128]{2,1,0:T(8,128)S(1)}, u32[]{:S(2)}) copy-start(f32[36,8,128]{2,1,0:T(8,128)S(1)} %collective-permute-done.4.zp_ref) | copy-start | bytes 442372
  39.9 0.7 copy-start.4
  42.5 8.0 %collective-permute-start.6 = (f32[17,8,128]{2,1,0:T(8,128)}, f32[17,8,128]{2,1,0:T(8,128)S(1)}, u32[]{:S(2)}, u32[]{:S(2)}) collective-permute-start(f32[17,8,128]{2,1,0:T(8,128)} %shard_map.43), channel_id=1, source_target_pairs={{0,1},{1,2},{2,3},{3,4},{4,5},{5,6},{6,7},{8,9},{9,10},{10,11},{11... | collective-permute-start | bytes 208904 | tf_op jit(solution)/shard_map/ppermute | solution.py:310
  48.5 5.8 %collective-permute-start.7 = (f32[17,8,128]{2,1,0:T(8,128)}, f32[17,8,128]{2,1,0:T(8,128)S(1)}, u32[]{:S(2)}, u32[]{:S(2)}) collective-permute-start(f32[17,8,128]{2,1,0:T(8,128)} %shard_map.43), channel_id=1, source_target_pairs={{1,0},{2,1},{3,2},{4,3},{5,4},{6,5},{7,6},{9,8},{10,9},{11,10},{12... | collective-permute-start | bytes 208904 | tf_op jit(solution)/shard_map/ppermute | solution.py:311
  54.4 0.9 copy-start.3
  55.3 0.9 copy-start.5

commit v2 on v1

--- a/solution.py
+++ b/solution.py
@@ -7,6 +7,7 @@
 from jax.experimental.pallas import tpu as pltpu
 from jax.sharding import PartitionSpec as P
 
+
 SIG = 0.28
 TAU = 0.28
 
@@ -15,8 +16,8 @@
 NTE = 17
 NF = 10
 NL = 8
-LW = 3
-LOFF = 64
+NP = NF + NL
+LW = 6
 
 
 def iota(axis):
@@ -34,47 +35,78 @@
 def lanes_of(lane, planes):
     hit = None
     for p in planes:
-        for base in (0, LOFF):
-            here = (lane >= base + LW * p) & (lane < base + LW * p + LW)
-            hit = here if hit is None else hit | here
+        here = (lane >= LW * p) & (lane < LW * p + LW)
+        hit = here if hit is None else hit | here
     return hit
 
 
-def pack_kernel(f_ref, l_ref, s_ref, up_ref, dn_ref):
+def strip_of(lane, acc, p, first, last):
+    both = pltpu.roll(jnp.where(lane < 64, first, last), (LW * p - 125) % 128, 1)
+    return jnp.where((lane >= LW * p) & (lane < LW * p + LW), both, acc)
+
+
+def pack_kernel(f_hbm, l_hbm, own_ref, z_ref, on_ref, back_ref, up_ref, dn_ref, fv, lv, sems):
     sub, lane = iota(0), iota(1)
+    copies = []
+    for t in range(FR):
+        for k, (src, dst) in enumerate(((f_hbm, fv), (l_hbm, lv))):
+            copies.append(pltpu.make_async_copy(src.at[t], dst.at[t], sems.at[2 * t + k]))
+            copies[-1].start()
+    for copy in copies:
+        copy.wait()
     for i in range(NT):
         acc = jnp.zeros((8, 128), jnp.float32)
         for t in range(FR):
-            for ref, p in ((f_ref, t + 3), (l_ref, t + 12)):
-                right = pltpu.roll(tile(ref, t, i, 1), (LW * p - 125) % 128, 1)
-                left = pltpu.roll(tile(ref, t, i, 0), (LOFF + LW * p) % 128, 1)
-                acc = jnp.where((lane >= LW * p) & (lane < LW * p + LW), right, acc)
-                acc = jnp.where((lane >= LOFF + LW * p) & (lane < LOFF + LW * p + LW), left, acc)
-        s_ref[i] = acc
+            acc = strip_of(lane, acc, t + 3, tile(fv, t, i, 0), tile(fv, t, i, 1))
+            acc = strip_of(lane, acc, t + 12, tile(lv, t, i, 0), tile(lv, t, i, 1))
+        own_ref[i] = acc
+        on_ref[i] = acc
+        back_ref[i] = acc
     for t in range(FR):
-        for k, ref in ((0, f_ref), (4, l_ref)):
+        for k, ref in ((0, fv), (1, lv)):
             for j in range(2):
-                s_ref[NT + 2 * (t + k) + j] = jnp.where(sub < 4, tile(ref, t, 0, j), tile(ref, t, NT - 1, j))
-    up_ref[0:3] = f_ref[1:4]
-    up_ref[3:5] = l_ref[2:4]
-    dn_ref[0:3] = f_ref[0:3]
-    dn_ref[3:5] = l_ref[0:2]
-
-
-def rows_kernel(own_ref, prev_ref, next_ref, z_ref):
-    def move(src, plane, dst):
+                z = jnp.where(sub < 4, tile(ref, t, 0, j), tile(ref, t, NT - 1, j))
+                z_ref[2 * (t + 4 * k) + j] = z
+                o = t - 1 if k == 0 else t + 1
+                if (k == 0 and t >= 1) or (k == 1 and t >= 2):
+                    on_ref[NT + 2 * o + j] = z
+                o = t if k == 0 else t + 3
+                if (k == 0 and t < 3) or (k == 1 and t < 2):
+                    back_ref[NT + 2 * o + j] = z
+    up_ref[0:3] = fv[1:4]
+    up_ref[3:5] = lv[2:4]
+    dn_ref[0:3] = fv[0:3]
+    dn_ref[3:5] = lv[0:2]
+
+
+def rows_kernel(z_ref, prev_ref, next_ref, on_ref, back_ref):
+    sub = iota(0)
+
+    def plane(p, j):
+        if p < 3:
+            return prev_ref[NT + 2 * p + j]
+        if p < 7:
+            return z_ref[2 * (p - 3) + j]
+        if p < 10:
+            return next_ref[NT + 2 * (p - 7) + j]
+        if p < 12:
+            return prev_ref[NT + 2 * (p - 7) + j]
+        if p < 16:
+            return z_ref[2 * (p - 8) + j]
+        return next_ref[NT + 2 * (p - 13) + j]
+
+    for m in range(NP // 2):
         for j in range(2):
-            z_ref[2 * dst + j] = src[NT + 2 * plane + j]
-
-    for k in range(3):
-        move(prev_ref, k + 1, k)
-        move(next_ref, k, 7 + k)
-    for k in range(4):
-        move(own_ref, k, 3 + k)
-        move(own_ref, 4 + k, 12 + k)
-    for k in range(2):
-        move(prev_ref, 6 + k, 10 + k)
-        move(next_ref, 4 + k, 16 + k)
+            a, b = plane(2 * m, j), pltpu.roll(plane(2 * m + 1, j), 4, 0)
+            on_ref[2 * m + j] = jnp.where(sub < 4, b, a)
+            back_ref[2 * m + j] = jnp.where(sub < 4, a, b)
+
+
+def halo_rows(sub, prev_ref, next_ref, p, j):
+    a, b = prev_ref[2 * (p // 2) + j], next_ref[2 * (p // 2) + j]
+    if p % 2 == 0:
+        return jnp.where(sub < 4, b, a)
+    return pltpu.roll(jnp.where(sub < 4, a, b), 4, 0)
 
 
 def cols_kernel(own_ref, prev_ref, next_ref, zp_ref, zn_ref, m_ref):
@@ -82,24 +114,19 @@
     from_prev = lanes_of(lane, (0, 1, 2, 10, 11))
     from_next = lanes_of(lane, (7, 8, 9, 16, 17))
     for i in range(NT):
-        a = pltpu.roll(prev_ref[i], 128 - 12, 1)
-        b = pltpu.roll(next_ref[i], 12, 1)
+        a = pltpu.roll(prev_ref[i], 128 - 4 * LW, 1)
+        b = pltpu.roll(next_ref[i], 4 * LW, 1)
         m_ref[i] = jnp.where(from_prev, a, jnp.where(from_next, b, own_ref[i]))
     acc = jnp.zeros((8, 128), jnp.float32)
-    for p in range(NF + NL):
-        left = jnp.where(sub < 4, zn_ref[2 * p], zp_ref[2 * p])
-        right = jnp.where(sub < 4, zn_ref[2 * p + 1], zp_ref[2 * p + 1])
-        right = pltpu.roll(right, (LW * p - 125) % 128, 1)
-        left = pltpu.roll(left, (LOFF + LW * p) % 128, 1)
-        acc = jnp.where((lane >= LW * p) & (lane < LW * p + LW), right, acc)
-        acc = jnp.where((lane >= LOFF + LW * p) & (lane < LOFF + LW * p + LW), left, acc)
+    for p in range(NP):
+        acc = strip_of(lane, acc, p, halo_rows(sub, zp_ref, zn_ref, p, 0), halo_rows(sub, zp_ref, zn_ref, p, 1))
     m_ref[NT] = acc
 
 
 def main_kernel(
     sizes, f_ref, l_ref, bp_ref, bn_ref, zp_ref, zn_ref, mp_ref, mn_ref,
-    out_ref, sum_ref,
-    ua, ub, qa, qb, v1, v2, wt, at, il, g1, g2,
+    out_hbm, sum_ref,
+    ua, ub, qa, qb, v1, v2, wt, at, il, g1, g2, out_ref, sems,
 ):
     n_tm, n_row, n_col = sizes
     sub, lane = iota(0), iota(1)
@@ -156,9 +183,9 @@
         return c
 
     lax.fori_loop(0, 2, face_lam, 0)
-    for p in range(NF + NL):
+    for p in range(NP):
         for j in range(2):
-            z = jnp.where(sub < 4, zn_ref[2 * p + j], zp_ref[2 * p + j])
+            z = halo_rows(sub, zp_ref, zn_ref, p, j)
             if p < NF:
                 put(ua, p, NT, j, z)
             else:
@@ -166,14 +193,15 @@
                 put(wt, p - NF, NT, j, w)
                 put(at, p - NF, NT, j, a)
 
+    from_left = lane % LW < 3
+    beside = (lane < 3) | (lane >= 125)
+
     def side(i, c):
         rows = pl.ds(pl.multiple_of(i * 8, 8), 8)
-        mp, mn = mp_ref[i], mn_ref[i]
+        strips = jnp.where(from_left, mp_ref[i], mn_ref[i])
         noisy = []
-        for p in range(NF + NL):
-            right = pltpu.roll(mn, (-(LOFF + LW * p)) % 128, 1)
-            left = pltpu.roll(mp, (125 - LW * p) % 128, 1)
-            x = jnp.where(lane < 3, right, jnp.where(lane >= 125, left, 0.0))
+        for p in range(NP):
+            x = jnp.where(beside, pltpu.roll(strips, (125 - LW * p) % 128, 1), 0.0)
             if p < NF:
                 ua[p, rows, 256:384] = x
                 noisy.append(x)
@@ -249,6 +277,9 @@
                     acc[j] = acc[j] + term
             before = rows
 
+    def leave(t):
+        return pltpu.make_async_copy(out_ref.at[t], out_hbm.at[t], sems.at[t])
+
     def run(step, u, uo, qi, qo, vi, vo, gi, go):
         lo, hi = step, 8 - step
 
@@ -268,6 +299,8 @@
         def primal_in(tt, c):
             acc = list(c)
             primal_step(step, u, qo, vi, vo, uo, tt, acc)
+            if step == 2:
+                leave(tt - 3).start()
             return tuple(acc)
 
         blank = jnp.zeros((8, 128), jnp.float32)
@@ -284,17 +317,20 @@
     total = [jnp.sum(s) for s in (s0, s1, s2)]
     col = lax.broadcasted_iota(jnp.int32, sum_ref.shape, 1)
     sum_ref[...] = jnp.where(col == 0, total[0], jnp.where(col == 1, total[1], jnp.where(col == 2, total[2], 0.0)))
+    for t in range(FR):
+        leave(t).wait()
 
 
 VMEM = pl.BlockSpec(memory_space=pltpu.VMEM)
-
-
-def call(kernel, outs, *args, flops, scratch=(), limit=None):
+HBM = pl.BlockSpec(memory_space=pltpu.HBM)
+
+
+def call(kernel, outs, *args, flops, scratch=(), limit=8 << 20, ins=None, places=None):
     return pl.pallas_call(
         kernel,
         out_shape=outs,
-        in_specs=[VMEM] * len(args),
-        out_specs=jax.tree.map(lambda _: VMEM, outs),
+        in_specs=ins or [VMEM] * len(args),
+        out_specs=places or jax.tree.map(lambda _: VMEM, outs),
         scratch_shapes=scratch,
         cost_estimate=pl.CostEstimate(flops=flops, bytes_accessed=1 << 20, transcendentals=0),
         compiler_params=pltpu.CompilerParams(vmem_limit_bytes=limit),
@@ -305,40 +341,49 @@
     return jax.ShapeDtypeStruct(shape, jnp.float32)
 
 
-def both_ways(later, earlier, axis):
+def both_ways(later, earlier, axis, ring=False):
     n = lax.axis_size(axis)
-    onward = lax.ppermute(later, axis, [(i, i + 1) for i in range(n - 1)])
-    back = lax.ppermute(earlier, axis, [(i + 1, i) for i in range(n - 1)])
+    pairs = [(i, (i + 1) % n) for i in range(n if ring else n - 1)]
+    onward = lax.ppermute(later, axis, pairs)
+    back = lax.ppermute(earlier, axis, [(b, a) for a, b in pairs])
     return onward, back
+
+
+def spread_sum(part, axes):
+    n = lax.axis_size(axes)
+    rows = jnp.broadcast_to(part, (n, 128))
+    return jnp.sum(lax.all_to_all(rows, axes, 0, 0, tiled=True), 0, keepdims=True)
 
 
 def on_device(noisy, lam):
     n_tm, n_row, n_col = (lax.axis_size(a) for a in ("tm", "row", "col"))
     cells = float(noisy.size * n_tm * n_row * n_col)
-    strip, up, down = call(
-        pack_kernel, (f32(NT + 16, 8, 128), f32(5, 128, 256), f32(5, 128, 256)), noisy, lam, flops=1 << 20
-    )
-    sp, sn = both_ways(strip, strip, "tm")
-    up, down, _, _ = lax.optimization_barrier((up, down, strip, strip))
-    bp, bn = both_ways(up, down, "tm")
-    z = call(rows_kernel, f32(2 * (NF + NL), 8, 128), strip, sp, sn, flops=1 << 20)
-    zp, zn = both_ways(z, z, "row")
-    m = call(cols_kernel, f32(NTE, 8, 128), strip, sp, sn, zp, zn, flops=1 << 20)
-    mp, mn = both_ways(m, m, "col")
     ext = lambda n: pltpu.VMEM((n, NTE * 8, 384), jnp.float32)
     inner = lambda n: pltpu.VMEM((n, 128, 256), jnp.float32)
-    out, rows = call(
+    strip, z, s_on, s_back, up, down = call(
+        pack_kernel,
+        (f32(NT, 8, 128), f32(16, 8, 128), f32(NT + 10, 8, 128), f32(NT + 10, 8, 128), f32(5, 128, 256), f32(5, 128, 256)),
+        pltpu.with_memory_space_constraint(noisy, pltpu.HBM), pltpu.with_memory_space_constraint(lam, pltpu.HBM),
+        flops=1 << 20, ins=[HBM, HBM], limit=8 << 20,
+        scratch=[inner(FR), inner(FR), pltpu.SemaphoreType.DMA((2 * FR,))],
+    )
+    sp, sn = both_ways(s_on, s_back, "tm")
+    bp, bn = both_ways(up, down, "tm")
+    z_on, z_back = call(rows_kernel, (f32(NP, 8, 128), f32(NP, 8, 128)), z, sp, sn, flops=1 << 20)
+    zp, zn = both_ways(z_on, z_back, "row")
+    m = call(cols_kernel, f32(NTE, 8, 128), strip, sp, sn, zp, zn, flops=1 << 20)
+    mp, mn = both_ways(m, m, "col", ring=True)
+    out, part = call(
         functools.partial(main_kernel, (n_tm, n_row, n_col)),
-        (f32(4, 128, 256), f32(n_row, 128)),
+        (f32(4, 128, 256), f32(n_tm * n_col, 128)),
         noisy, lam, bp, bn, zp, zn, mp, mn,
-        flops=1 << 26,
-        scratch=[ext(NF), ext(NF), ext(3 * NF), ext(3 * NF), ext(NF), ext(NF), ext(NL), ext(NL), inner(4), inner(12), inner(12)],
+        flops=1 << 26, places=(HBM, VMEM),
+        scratch=[ext(NF), ext(NF), ext(3 * NF), ext(3 * NF), ext(NF), ext(NF), ext(NL), ext(NL), inner(4), inner(12), inner(12)]
+        + [inner(FR), pltpu.SemaphoreType.DMA((FR,))],
         limit=40 << 20,
     )
-    part = jnp.sum(lax.all_to_all(rows, "row", 0, 0, tiled=True), 0, keepdims=True)
-    part = jnp.broadcast_to(part, (n_tm * n_col, 128))
-    part = jnp.sum(lax.all_to_all(part, ("tm", "col"), 0, 0, tiled=True), 0)
-    gaps = part[:3] / cells
+    part = jnp.sum(lax.all_to_all(part, ("tm", "col"), 0, 0, tiled=True), 0, keepdims=True)
+    gaps = spread_sum(part, "row")[0, :3] / cells
     return out, gaps
 
 

time: 108 us -> 92.7 us (0.86)
  Pallas kernels: 17.1 us -> 12.2 us
  starting transfers between devices: 26.7 us -> 23 us
  waiting for transfers between devices: 19.4 us -> 15.7 us
  local copies, waits for them, and re-layouts: 3.15 us -> 0.02 us
    pallas_call x4, Pallas kernels: 17.1 us -> 12.2 us  [call(): pl.pallas_call(kernel, out_shape=outs, in_specs=ins or [VMEM] * len(args)...]
    ppermute x8, starting transfers between devices: 26.7 us -> 23 us  [the longest x4 16 us: both_ways(): onward = lax.ppermute(later, axis, pairs)]
    ppermute x8, waiting for transfers between devices: 19.4 us -> 15.7 us  [the longest x4 9.73 us: both_ways(): back = lax.ppermute(earlier, axis, [(b, a) for a, b in pairs])]
    unnamed x16 -> x4, local copies, waits for them, and re-layouts: 3.14 us -> 0.01 us
  transfers between devices with their start and end apart: 8 -> 8, of which waited for: 5 -> 5; matrix products, arithmetic and copies ran while one was open for 0% -> 0% of each run, Pallas kernels for 3% -> 0%
where the time goes in v2:
time: 92.7 us; the launch traced here: 92.3 us
  blocking collectives  40.1 us (43%)
  starting transfers between devices  23 us (25%)
  waiting for transfers between devices  15.7 us (17%)
  Pallas kernels  12.2 us (13%)
    all_to_all x1, blocking collectives, spread_sum(): lax.all_to_all(rows, axes, 0, 0, tiled=True)  25.9 us
    ppermute x4, starting transfers between devices, both_ways(): onward = lax.ppermute(later, axis, pairs)  16 us
    all_to_all x1, blocking collectives, on_device(): lax.all_to_all(part, ('tm', 'col'), 0, 0, tiled=True)  14.2 us
    pallas_call x4, Pallas kernels, call(): pl.pallas_call(kernel, out_shape=outs, in_specs=ins or [VMEM] * len(args)...  12.2 us
    ppermute x4, waiting for transfers between devices, both_ways(): back = lax.ppermute(earlier, axis, [(b, a) for a, b in pairs])  9.73 us
    ppermute x4, starting transfers between devices, both_ways(): back = lax.ppermute(earlier, axis, [(b, a) for a, b in pairs])  6.94 us
    ppermute x4, waiting for transfers between devices, both_ways(): onward = lax.ppermute(later, axis, pairs)  5.98 us
  transfers between devices with their start and end apart: 8, of which 5 were waited for; matrix products, arithmetic and copies ran while one was open for 0% of the time, Pallas kernels for 0%

profile of v2, /device:TPU:1, one launch (start us, length us, event | category | flops | bytes accessed | tf_op | source)
XLA Modules:
  0.0 92.3 jit_solution(811926266142340192)
XLA Ops:
  0.6 0.0 copy-start.1
  0.6 1.7 %shard_map.41 = (f32[16,8,128]{2,1,0:T(8,128)S(1)}, f32[16,8,128]{2,1,0:T(8,128)S(1)}, f32[26,8,128]{2,1,0:T(8,128)S(1)}, f32[26,8,128]{2,1,0:T(8,128)S(1)}, f32...) custom-call(f32[4,128,256]{2,1,0:T(8,128)} %f_ref.1, f32[4,128,256]{2,1,0:T(8,128)} %l_ref.1), custom_call_target="tpu_custom_call" | custom-call | flops 1048576 | bytes 1048576 | tf_op jit(solution)/shard_map/pallas_call | solution.py:329
  2.3 0.0 copy-start
  2.4 4.2 %collective-permute-start = (f32[5,128,256]{2,1,0:T(8,128)S(1)}, f32[5,128,256]{2,1,0:T(8,128)S(1)}, u32[]{:S(2)}, u32[]{:S(2)}) collective-permute-start(f32[5,128,256]{2,1,0:T(8,128)S(1)} %get-tuple-element.12), channel_id=1, source_target_pairs={{0,128},{128,256},{256,384},{1,129},{129,257},{257,385},{2,130},{1... | collective-permute-start | bytes 1966088 | tf_op jit(solution)/shard_map/ppermute | solution.py:347
  6.6 1.3 %collective-permute-start.1 = (f32[5,128,256]{2,1,0:T(8,128)S(1)}, f32[5,128,256]{2,1,0:T(8,128)S(1)}, u32[]{:S(2)}, u32[]{:S(2)}) collective-permute-start(f32[5,128,256]{2,1,0:T(8,128)S(1)} %get-tuple-element.13), channel_id=1, source_target_pairs={{128,0},{256,128},{384,256},{129,1},{257,129},{385,257},{130,2},{2... | collective-permute-start | bytes 1966088 | tf_op jit(solution)/shard_map/ppermute | solution.py:348
  7.9 4.0 %collective-permute-start.2 = (f32[26,8,128]{2,1,0:T(8,128)S(1)}, f32[26,8,128]{2,1,0:T(8,128)S(1)}, u32[]{:S(2)}, u32[]{:S(2)}) collective-permute-start(f32[26,8,128]{2,1,0:T(8,128)S(1)} %get-tuple-element.15), channel_id=1, source_target_pairs={{0,128},{128,256},{256,384},{1,129},{129,257},{257,385},{2,130},{1... | collective-permute-start | bytes 319496 | tf_op jit(solution)/shard_map/ppermute | solution.py:347
  11.9 1.3 %collective-permute-start.3 = (f32[26,8,128]{2,1,0:T(8,128)S(1)}, f32[26,8,128]{2,1,0:T(8,128)S(1)}, u32[]{:S(2)}, u32[]{:S(2)}) collective-permute-start(f32[26,8,128]{2,1,0:T(8,128)S(1)} %get-tuple-element.16), channel_id=1, source_target_pairs={{128,0},{256,128},{384,256},{129,1},{257,129},{385,257},{130,2},{2... | collective-permute-start | bytes 319496 | tf_op jit(solution)/shard_map/ppermute | solution.py:348
  13.2 5.9 %collective-permute-done.2.prev_ref = f32[26,8,128]{2,1,0:T(8,128)S(1)} collective-permute-done((f32[26,8,128]{2,1,0:T(8,128)S(1)}, f32[26,8,128]{2,1,0:T(8,128)S(1)}, u32[]{:S(2)}, u32[]{:S(2)}) %collective-permute-start.2) | collective-permute-done | bytes 106528 | tf_op jit(solution)/shard_map/ppermute | solution.py:347
  19.0 3.9 %collective-permute-done.3.next_ref = f32[26,8,128]{2,1,0:T(8,128)S(1)} collective-permute-done((f32[26,8,128]{2,1,0:T(8,128)S(1)}, f32[26,8,128]{2,1,0:T(8,128)S(1)}, u32[]{:S(2)}, u32[]{:S(2)}) %collective-permute-start.3) | collective-permute-done | bytes 106528 | tf_op jit(solution)/shard_map/ppermute | solution.py:348
  22.9 6.7 %collective-permute-start.4 = (f32[18,8,128]{2,1,0:T(8,128)S(1)}, f32[18,8,128]{2,1,0:T(8,128)S(1)}, u32[]{:S(2)}, u32[]{:S(2)}) collective-permute-start(f32[18,8,128]{2,1,0:T(8,128)S(1)} %get-tuple-element.17), channel_id=1, source_target_pairs={{0,8},{8,16},{16,24},{24,32},{32,40},{40,48},{48,56},{56,64},{64,7... | collective-permute-start | bytes 221192 | tf_op jit(solution)/shard_map/ppermute | solution.py:347
  29.6 1.3 %collective-permute-start.5 = (f32[18,8,128]{2,1,0:T(8,128)S(1)}, f32[18,8,128]{2,1,0:T(8,128)S(1)}, u32[]{:S(2)}, u32[]{:S(2)}) collective-permute-start(f32[18,8,128]{2,1,0:T(8,128)S(1)} %get-tuple-element.18), channel_id=1, source_target_pairs={{8,0},{16,8},{24,16},{32,24},{40,32},{48,40},{56,48},{64,56},{72,6... | collective-permute-start | bytes 221192 | tf_op jit(solution)/shard_map/ppermute | solution.py:348
  30.9 0.1 collective-permute-done.4.zp_ref
  31.0 3.9 %collective-permute-done.5.zn_ref = f32[18,8,128]{2,1,0:T(8,128)S(1)} collective-permute-done((f32[18,8,128]{2,1,0:T(8,128)S(1)}, f32[18,8,128]{2,1,0:T(8,128)S(1)}, u32[]{:S(2)}, u32[]{:S(2)}) %collective-permute-start.5) | collective-permute-done | bytes 73760 | tf_op jit(solution)/shard_map/ppermute | solution.py:348
  34.9 0.1 shard_map.43
  35.0 3.1 %collective-permute-start.7 = (f32[17,8,128]{2,1,0:T(8,128)S(1)}, f32[17,8,128]{2,1,0:T(8,128)S(1)}, u32[]{:S(2)}, u32[]{:S(2)}) collective-permute-start(f32[17,8,128]{2,1,0:T(8,128)S(1)} %shard_map.43), channel_id=1, source_target_pairs={{1,0},{2,1},{3,2},{4,3},{5,4},{6,5},{7,6},{0,7},{9,8},{10,9},{11,1... | collective-permute-start | bytes 208904 | tf_op jit(solution)/shard_map/ppermute | solution.py:348
  38.1 1.1 %collective-permute-start.6 = (f32[17,8,128]{2,1,0:T(8,128)S(1)}, f32[17,8,128]{2,1,0:T(8,128)S(1)}, u32[]{:S(2)}, u32[]{:S(2)}) collective-permute-start(f32[17,8,128]{2,1,0:T(8,128)S(1)} %shard_map.43), channel_id=1, source_target_pairs={{0,1},{1,2},{2,3},{3,4},{4,5},{5,6},{6,7},{7,0},{8,9},{9,10},{10,1... | collective-permute-start | bytes 208904 | tf_op jit(solution)/shard_map/ppermute | solution.py:347
  39.2 2.0 %collective-permute-done.7.mn_ref = f32[17,8,128]{2,1,0:T(8,128)S(1)} collective-permute-done((f32[17,8,128]{2,1,0:T(8,128)S(1)}, f32[17,8,128]{2,1,0:T(8,128)S(1)}, u32[]{:S(2)}, u32[]{:S(2)}) %collective-permute-start.7) | collective-permute-done | bytes 69664 | tf_op jit(solution)/shard_map/ppermute | solution.py:348
  41.2 0.0 collective-permute-done.6.mp_ref
  41.2 0.0 collective-permute-done.bp_ref
  41.2 0.0 collective-permute-done.1.bn_ref
  41.2 0.0 copy-done.1
  41.2 0.0 copy-done
  41.2 10.4 %shard_map.44 = (f32[4,128,256]{2,1,0:T(8,128)}, f32[32,128]{1,0:T(8,128)S(1)}) custom-call(f32[4,128,256]{2,1,0:T(8,128)S(1)} %copy-done, f32[4,128,256]{2,1,0:T(8,128)S(1)} %copy-done.1, f32[5,128,256]{2,1,0:T(8,128)S(1)} %collective-permute-done.bp_ref, f32[5,128,256]{2,1,0:T(8,128)S(1)} %collective-permute-done.1.bn_ref, ...), custom_call_target="tpu_custom_call" | custom-call | flops 67108864 | bytes 1048576 | tf_op jit(solution)/shard_map/pallas_call | solution.py:329
  51.7 14.2 %all_to_all.15 = f32[32,1,128]{2,1,0:T(1,128)S(1)} all-to-all(f32[32,1,128]{2,1,0:T(1,128)S(1)} %bitcast.7), channel_id=1, replica_groups=mesh['tm'=4,'row'=16,'col'=8] {'tm','col'}, dimensions={0} | all-to-all | bytes 32768 | tf_op jit(solution)/shard_map/all_to_all | solution.py:385
  65.8 0.1 reduce_sum.18
  65.9 25.9 %all_to_all.16 = f32[16,1,128]{2,1,0:T(1,128)S(1)} all-to-all(f32[16,1,128]{2,1,0:T(1,128)S(1)} %broadcast_in_dim.4), channel_id=1, replica_groups=mesh['tm'=4,'row'=16,'col'=8] {'row'}, dimensions={0} | all-to-all | bytes 16384 | tf_op jit(solution)/shard_map/all_to_all | solution.py:355
  91.8 0.5 multiply_bitcast_fusion
  (3 shorter events, 0.0 us)
Async XLA Ops:
  0.6 40.6 %copy-start.1 = (f32[4,128,256]{2,1,0:T(8,128)S(1)}, f32[4,128,256]{2,1,0:T(8,128)}, u32[]{:S(2)}) copy-start(f32[4,128,256]{2,1,0:T(8,128)} %l_ref.1) | copy-start | bytes 1572868
  2.3 38.9 %copy-start = (f32[4,128,256]{2,1,0:T(8,128)S(1)}, f32[4,128,256]{2,1,0:T(8,128)}, u32[]{:S(2)}) copy-start(f32[4,128,256]{2,1,0:T(8,128)} %f_ref.1) | copy-start | bytes 1572868
  2.4 38.9 %collective-permute-start = (f32[5,128,256]{2,1,0:T(8,128)S(1)}, f32[5,128,256]{2,1,0:T(8,128)S(1)}, u32[]{:S(2)}, u32[]{:S(2)}) collective-permute-start(f32[5,128,256]{2,1,0:T(8,128)S(1)} %get-tuple-element.12), channel_id=1, source_target_pairs={{0,128},{128,256},{256,384},{1,129},{129,257},{257,385},{2,130},{1... | collective-permute-start | bytes 1966088 | tf_op jit(solution)/shard_map/ppermute | solution.py:347
  6.6 34.7 %collective-permute-start.1 = (f32[5,128,256]{2,1,0:T(8,128)S(1)}, f32[5,128,256]{2,1,0:T(8,128)S(1)}, u32[]{:S(2)}, u32[]{:S(2)}) collective-permute-start(f32[5,128,256]{2,1,0:T(8,128)S(1)} %get-tuple-element.13), channel_id=1, source_target_pairs={{128,0},{256,128},{384,256},{129,1},{257,129},{385,257},{130,2},{2... | collective-permute-start | bytes 1966088 | tf_op jit(solution)/shard_map/ppermute | solution.py:348
  7.9 11.2 %collective-permute-start.2 = (f32[26,8,128]{2,1,0:T(8,128)S(1)}, f32[26,8,128]{2,1,0:T(8,128)S(1)}, u32[]{:S(2)}, u32[]{:S(2)}) collective-permute-start(f32[26,8,128]{2,1,0:T(8,128)S(1)} %get-tuple-element.15), channel_id=1, source_target_pairs={{0,128},{128,256},{256,384},{1,129},{129,257},{257,385},{2,130},{1... | collective-permute-start | bytes 319496 | tf_op jit(solution)/shard_map/ppermute | solution.py:347
  11.9 11.1 %collective-permute-start.3 = (f32[26,8,128]{2,1,0:T(8,128)S(1)}, f32[26,8,128]{2,1,0:T(8,128)S(1)}, u32[]{:S(2)}, u32[]{:S(2)}) collective-permute-start(f32[26,8,128]{2,1,0:T(8,128)S(1)} %get-tuple-element.16), channel_id=1, source_target_pairs={{128,0},{256,128},{384,256},{129,1},{257,129},{385,257},{130,2},{2... | collective-permute-start | bytes 319496 | tf_op jit(solution)/shard_map/ppermute | solution.py:348
  22.9 8.1 %collective-permute-start.4 = (f32[18,8,128]{2,1,0:T(8,128)S(1)}, f32[18,8,128]{2,1,0:T(8,128)S(1)}, u32[]{:S(2)}, u32[]{:S(2)}) collective-permute-start(f32[18,8,128]{2,1,0:T(8,128)S(1)} %get-tuple-element.17), channel_id=1, source_target_pairs={{0,8},{8,16},{16,24},{24,32},{32,40},{40,48},{48,56},{56,64},{64,7... | collective-permute-start | bytes 221192 | tf_op jit(solution)/shard_map/ppermute | solution.py:347
  29.6 5.3 %collective-permute-start.5 = (f32[18,8,128]{2,1,0:T(8,128)S(1)}, f32[18,8,128]{2,1,0:T(8,128)S(1)}, u32[]{:S(2)}, u32[]{:S(2)}) collective-permute-start(f32[18,8,128]{2,1,0:T(8,128)S(1)} %get-tuple-element.18), channel_id=1, source_target_pairs={{8,0},{16,8},{24,16},{32,24},{40,32},{48,40},{56,48},{64,56},{72,6... | collective-permute-start | bytes 221192 | tf_op jit(solution)/shard_map/ppermute | solution.py:348
  35.0 6.2 %collective-permute-start.7 = (f32[17,8,128]{2,1,0:T(8,128)S(1)}, f32[17,8,128]{2,1,0:T(8,128)S(1)}, u32[]{:S(2)}, u32[]{:S(2)}) collective-permute-start(f32[17,8,128]{2,1,0:T(8,128)S(1)} %shard_map.43), channel_id=1, source_target_pairs={{1,0},{2,1},{3,2},{4,3},{5,4},{6,5},{7,6},{0,7},{9,8},{10,9},{11,1... | collective-permute-start | bytes 208904 | tf_op jit(solution)/shard_map/ppermute | solution.py:348
  38.1 3.1 %collective-permute-start.6 = (f32[17,8,128]{2,1,0:T(8,128)S(1)}, f32[17,8,128]{2,1,0:T(8,128)S(1)}, u32[]{:S(2)}, u32[]{:S(2)}) collective-permute-start(f32[17,8,128]{2,1,0:T(8,128)S(1)} %shard_map.43), channel_id=1, source_target_pairs={{0,1},{1,2},{2,3},{3,4},{4,5},{5,6},{6,7},{7,0},{8,9},{9,10},{10,1... | collective-permute-start | bytes 208904 | tf_op jit(solution)/shard_map/ppermute | solution.py:347

commit v3 on v2

v3 whole, which is shorter than its diff:
```python
import functools

import jax
import jax.numpy as jnp
from jax import lax
from jax.experimental import pallas as pl
from jax.experimental.pallas import tpu as pltpu
from jax.sharding import PartitionSpec as P


SIG = 0.28
TAU = 0.28

FR = 4
NT = 16
NTE = 17
NF = 10
NL = 8
NP = NF + NL
LW = 6


def iota(axis):
    return lax.broadcasted_iota(jnp.int32, (8, 128), axis)


def tile(ref, lead, i, j):
    return ref[lead, i * 8 : (i + 1) * 8, j * 128 : (j + 1) * 128]


def put(ref, lead, i, j, value):
    ref[lead, i * 8 : (i + 1) * 8, j * 128 : (j + 1) * 128] = value


def xtile(ref, lead, i, j):
    return ref[lead, 3 * i + j]


def xput(ref, lead, i, j, value):
    ref[lead, 3 * i + j] = value


def size_of(square):
    return square * lax.rsqrt(jnp.maximum(square, 1e-37))


def strip_of(lane, acc, p, first, last):
    both = pltpu.roll(jnp.where(lane < 64, first, last), (LW * p - 125) % 128, 1)
    return jnp.where((lane >= LW * p) & (lane < LW * p + LW), both, acc)


ZO = NT // 4


def gather4(lane, acc, strip, g, noisy_at, lam_at):
    a = pltpu.roll(strip, (32 * g - LW * noisy_at) % 128, 1)
    b = pltpu.roll(strip, (32 * g + 3 * LW - LW * lam_at) % 128, 1)
    acc = jnp.where((lane >= 32 * g) & (lane < 32 * g + 3 * LW), a, acc)
    return jnp.where((lane >= 32 * g + 3 * LW) & (lane < 32 * g + 5 * LW), b, acc)


def spread4(lane, acc, strips, g, noisy_at, lam_at):
    a = pltpu.roll(strips, (LW * noisy_at - 32 * g) % 128, 1)
    b = pltpu.roll(strips, (LW * lam_at - 32 * g - 3 * LW) % 128, 1)
    acc = jnp.where((lane >= LW * noisy_at) & (lane < LW * noisy_at + 3 * LW), a, acc)
    return jnp.where((lane >= LW * lam_at) & (lane < LW * lam_at + 2 * LW), b, acc)


def pack_kernel(f_hbm, l_hbm, own_ref, z_ref, on_ref, back_ref, up_ref, dn_ref, fv, lv, sems):
    sub, lane = iota(0), iota(1)
    copies = []
    for t in range(FR):
        for k, (src, dst) in enumerate(((f_hbm, fv), (l_hbm, lv))):
            copies.append(pltpu.make_async_copy(src.at[t], dst.at[t], sems.at[2 * t + k]))
            copies[-1].start()
    blank = jnp.zeros((8, 128), jnp.float32)
    strips = [blank] * NT
    for t in range(FR):
        copies[2 * t].wait()
        copies[2 * t + 1].wait()
        for i in range(NT):
            for ref, p in ((fv, t + 3), (lv, t + 12)):
                strips[i] = strip_of(lane, strips[i], p, tile(ref, t, i, 0), tile(ref, t, i, 1))
        for k, ref in ((0, fv), (1, lv)):
            for j in range(2):
                z = jnp.where(sub < 4, tile(ref, t, 0, j), tile(ref, t, NT - 1, j))
                z_ref[2 * (t + 4 * k) + j] = z
                if t >= 1 + k:
                    on_ref[ZO + 2 * (t + 2 * k - 1) + j] = z
                if t < 3 - k:
                    back_ref[ZO + 2 * (t + 3 * k) + j] = z
        if t >= 1:
            up_ref[t - 1] = fv[t]
        if t >= 2:
            up_ref[t + 1] = lv[t]
        if t < 3:
            dn_ref[t] = fv[t]
        if t < 2:
            dn_ref[t + 3] = lv[t]
    for k in range(ZO):
        onward, back = blank, blank
        for g in range(4):
            onward = gather4(lane, onward, strips[4 * k + g], g, 4, 14)
            back = gather4(lane, back, strips[4 * k + g], g, 3, 12)
        on_ref[k] = onward
        back_ref[k] = back
    for i in range(NT):
        own_ref[i] = strips[i]


def rows_kernel(z_ref, prev_ref, next_ref, on_ref, back_ref):
    sub = iota(0)

    def plane(p, j):
        if p < 3:
            return prev_ref[ZO + 2 * p + j]
        if p < 7:
            return z_ref[2 * (p - 3) + j]
        if p < 10:
            return next_ref[ZO + 2 * (p - 7) + j]
        if p < 12:
            return prev_ref[ZO + 2 * (p - 7) + j]
        if p < 16:
            return z_ref[2 * (p - 8) + j]
        return next_ref[ZO + 2 * (p - 13) + j]

    for m in range(NP // 2):
        for j in range(2):
            a, b = plane(2 * m, j), pltpu.roll(plane(2 * m + 1, j), 4, 0)
            on_ref[2 * m + j] = jnp.where(sub < 4, b, a)
            back_ref[2 * m + j] = jnp.where(sub < 4, a, b)


def halo_rows(sub, prev_ref, next_ref, p, j):
    a, b = prev_ref[2 * (p // 2) + j], next_ref[2 * (p // 2) + j]
    if p % 2 == 0:
        return jnp.where(sub < 4, b, a)
    return pltpu.roll(jnp.where(sub < 4, a, b), 4, 0)


def cols_kernel(own_ref, prev_ref, next_ref, zp_ref, zn_ref, m_ref):
    sub, lane = iota(0), iota(1)
    for i in range(NT):
        m = spread4(lane, own_ref[i], prev_ref[i // 4], i % 4, 0, 10)
        m_ref[i] = spread4(lane, m, next_ref[i // 4], i % 4, 7, 16)
    acc = jnp.zeros((8, 128), jnp.float32)
    for p in range(NP):
        acc = strip_of(lane, acc, p, halo_rows(sub, zp_ref, zn_ref, p, 0), halo_rows(sub, zp_ref, zn_ref, p, 1))
    m_ref[NT] = acc


def prim(lam, noisy):
    scaled = TAU * lam
    return 1.0 / (1.0 + scaled), scaled * noisy


def steps_of(sizes, f_ref, l_ref, wt, at, il, out_ref):
    n_tm, n_row, n_col = sizes
    sub, lane = iota(0), iota(1)
    first_t = lax.axis_index("tm") == 0
    last_t = lax.axis_index("tm") == n_tm - 1
    one, zero = jnp.float32(1.0), jnp.float32(0.0)
    last_r = jnp.where(lax.axis_index("row") == n_row - 1, zero, one)
    first_r = jnp.where(lax.axis_index("row") == 0, zero, one)
    last_c = jnp.where(lax.axis_index("col") == n_col - 1, zero, one)
    first_c = jnp.where(lax.axis_index("col") == 0, zero, one)
    ones = jnp.ones((8, 128), jnp.float32)
    row_mask = {NT - 1: jnp.where(sub == 7, ones * last_r, ones), NT: jnp.where(sub == 7, ones * first_r, ones)}
    col_mask = {1: jnp.where(lane == 127, ones * last_c, ones), 2: jnp.where(lane == 127, ones * first_c, ones)}

    def dual_step(step, u, qi, qo, tt, gi, go, acc):
        inside = acc is not None
        keep = jnp.where(((tt == 6) & last_t) | ((tt == 2) & first_t), zero, one)
        here = [xtile(u, tt, 0, j) for j in range(3)]
        start = here
        for i in range(NTE):
            after = start if i == NT else [xtile(u, tt, i + 1, j) for j in range(3)]
            turned = [pltpu.roll(here[j], 127, 1) for j in range(3)]
            for j in range(3):
                x = here[j]
                d0 = (xtile(u, tt + 1, i, j) - x) * keep
                d1 = pltpu.roll(jnp.where(sub == 0, after[j], x), 7, 0) - x
                if i in row_mask:
                    d1 = d1 * row_mask[i]
                d2 = jnp.where(lane == 127, turned[(j + 1) % 3], turned[j]) - x
                if j in col_mask:
                    d2 = d2 * col_mask[j]
                d = (d0, d1, d2)
                if inside and i < NT and j < 2:
                    gu = d
                    t = tt - 3
                    if step > 0:
                        gu = tuple(0.5 * (d[k] + tile(gi, 4 * k + t, i, j)) for k in range(3))
                    if step < 2:
                        for k in range(3):
                            put(go, 4 * k + t, i, j, gu[k])
                    else:
                        acc[j] = acc[j] + size_of(gu[0] * gu[0] + gu[1] * gu[1] + gu[2] * gu[2])
                m = d if step == 0 else tuple(d[k] + xtile(qi, NF * k + tt, i, j) for k in range(3))
                n2 = (m[0] * m[0] + m[1] * m[1] + m[2] * m[2]) * (SIG * SIG)
                s = jnp.minimum(1.0, lax.rsqrt(n2))
                for k in range(3):
                    xput(qo, NF * k + tt, i, j, m[k] * s)
            here = after

    def primal_step(step, u, q, vi, vo, uo, tt, acc):
        inside = acc is not None
        nj = 3 if step < 2 else 2
        before = [xtile(q, NF + tt, NT, j) for j in range(nj)]
        for i in range(NTE if step < 2 else NT):
            rows = [xtile(q, NF + tt, i, j) for j in range(nj)]
            cols = [xtile(q, 2 * NF + tt, i, j) for j in range(3)]
            turned = [pltpu.roll(cols[j], 1, 1) for j in range(3)]
            for j in range(nj):
                d = xtile(q, tt, i, j) - xtile(q, tt - 1, i, j)
                d = d + (rows[j] - pltpu.roll(jnp.where(sub == 7, before[j], rows[j]), 1, 0))
                d = d + (cols[j] - jnp.where(lane == 0, turned[j - 1], turned[j]))
                old = xtile(u, tt, i, j) if step == 0 else xtile(vi, tt, i, j)
                new = (old + (TAU * SIG) * d + xtile(at, tt - 1, i, j)) * xtile(wt, tt - 1, i, j)
                if step < 2:
                    xput(vo, tt, i, j, new)
                    xput(uo, tt, i, j, 2.0 * new - old)
                else:
                    put(out_ref, tt - 3, i, j, new)
                if inside and i < NT and j < 2:
                    t = tt - 3
                    e = SIG * d
                    noisy = tile(f_ref, t, i, j)
                    term = e * (e * tile(il, t, i, j) + noisy)
                    if step > 0:
                        r = old - noisy
                        term = term + (0.5 * tile(l_ref, t, i, j)) * (r * r)
                    acc[j] = acc[j] + term
            before = rows

    return dual_step, primal_step


def prep_kernel(sizes, f_ref, l_ref, zp_ref, zn_ref, mp_ref, mn_ref, ua, ub, qa, v1, wt, at, g1, il, acc_ref):
    sub, lane = iota(0), iota(1)

    def fill_noisy(src, at0, dst):
        for i in range(NT):
            for j in range(2):
                xput(ua, dst, i, j, tile(src, at0, i, j))

    def own(t, c):
        fill_noisy(f_ref, t, t + 3)
        for i in range(NT):
            for j in range(2):
                lam = tile(l_ref, t, i, j)
                w, a = prim(lam, tile(f_ref, t, i, j))
                xput(wt, t + 2, i, j, w)
                xput(at, t + 2, i, j, a)
                put(il, t, i, j, 0.5 / lam)
        return c

    lax.fori_loop(0, FR, own, 0)

    for p in range(NP):
        for j in range(2):
            z = halo_rows(sub, zp_ref, zn_ref, p, j)
            if p < NF:
                xput(ua, p, NT, j, z)
            else:
                w, a = prim(z, xtile(ua, p - NF + 1, NT, j))
                xput(wt, p - NF, NT, j, w)
                xput(at, p - NF, NT, j, a)

    from_left = lane % LW < 3
    beside = (lane < 3) | (lane >= 125)

    def side(i, c):
        strips = jnp.where(from_left, mp_ref[i], mn_ref[i])
        noisy = []
        for p in range(NP):
            x = jnp.where(beside, pltpu.roll(strips, (125 - LW * p) % 128, 1), 0.0)
            if p < NF:
                xput(ua, p, i, 2, x)
                noisy.append(x)
            else:
                w, a = prim(x, noisy[p - NF + 1])
                xput(wt, p - NF, i, 2, w)
                xput(at, p - NF, i, 2, a)
        return c

    lax.fori_loop(0, NTE, side, 0)

    dual_step, primal_step = steps_of(sizes, f_ref, l_ref, wt, at, il, None)

    def dual_in(tt, c):
        dual_step(0, ua, None, qa, tt, None, g1, list(c))
        return c

    def primal_in(tt, c):
        acc = list(c)
        primal_step(0, ua, qa, None, v1, ub, tt, acc)
        return tuple(acc)

    blank = jnp.zeros((8, 128), jnp.float32)
    lax.fori_loop(3, 6, dual_in, (blank, blank))
    acc = lax.fori_loop(4, 6, primal_in, (blank, blank))
    acc_ref[...] = acc[0] + acc[1]


def main_kernel(
    sizes, f_ref, l_ref, bp_ref, bn_ref, il, acc_ref, *refs
):
    (out_hbm, sum_ref, ua, ub, qa, v1, wt, at, g1, qb, v2, g2, out_ref, sems) = refs[7:]
    lane = iota(1)

    def fill_noisy(src, at0, dst):
        for i in range(NT):
            for j in range(2):
                xput(ua, dst, i, j, tile(src, at0, i, j))

    def fill_lam(src, at0, dst):
        for i in range(NT):
            for j in range(2):
                w, a = prim(tile(src, at0, i, j), xtile(ua, dst + 1, i, j))
                xput(wt, dst, i, j, w)
                xput(at, dst, i, j, a)

    def face(k, c):
        fill_noisy(bp_ref, k, k)
        fill_noisy(bn_ref, k, k + 7)
        return c

    lax.fori_loop(0, 3, face, 0)

    def face_lam(k, c):
        fill_lam(bp_ref, 3 + k, k)
        fill_lam(bn_ref, 3 + k, 6 + k)
        return c

    lax.fori_loop(0, 2, face_lam, 0)
    dual_step, primal_step = steps_of(sizes, f_ref, l_ref, wt, at, il, out_ref)

    def leave(t):
        return pltpu.make_async_copy(out_ref.at[t], out_hbm.at[t], sems.at[t])

    def run(step, u, uo, qi, qo, vi, vo, gi, go):
        lo, hi = step, 8 - step

        def dual_out(k, c):
            dual_step(step, u, qi, qo, jnp.where(k < 3, k, k + 4), gi, go, None)
            return c

        def dual_in(tt, c):
            acc = list(c)
            dual_step(step, u, qi, qo, tt, gi, go, acc)
            return tuple(acc)

        def primal_out(k, c):
            primal_step(step, u, qo, vi, vo, uo, jnp.where(k < 3, k, k + 4), None)
            return c

        def primal_in(k, c):
            acc = list(c)
            tt = 3 + 3 * k if step == 0 else k
            primal_step(step, u, qo, vi, vo, uo, tt, acc)
            if step == 2:
                leave(tt - 3).start()
            return tuple(acc)

        blank = jnp.zeros((8, 128), jnp.float32)
        lax.fori_loop(lo, hi - 3, dual_out, 0)
        acc = lax.fori_loop(6 if step == 0 else 3, 7, dual_in, (blank, blank))
        if step < 2:
            lax.fori_loop(lo + 1, hi - 3, primal_out, 0)
        acc = lax.fori_loop(0 if step == 0 else 3, 2 if step == 0 else 7, primal_in, acc)
        return acc[0] + acc[1]

    s0 = acc_ref[...] + run(0, ua, ub, None, qa, None, v1, None, g1)
    s1 = run(1, ub, ua, qa, qb, v1, v2, g1, g2)
    s2 = run(2, ua, None, qb, qa, v2, None, g2, None)

    def variation(t, c):
        acc = list(c)
        for i in range(NT):
            for j in range(2):
                for k, g in enumerate((g1, g2)):
                    x = [tile(g, 4 * n + t, i, j) for n in range(3)]
                    acc[k] = acc[k] + size_of(x[0] * x[0] + x[1] * x[1] + x[2] * x[2])
        return tuple(acc)

    s0, s1 = lax.fori_loop(0, FR, variation, (s0, s1))
    total = [jnp.sum(s) for s in (s0, s1, s2)]
    col = lax.broadcasted_iota(jnp.int32, sum_ref.shape, 1)
    sum_ref[...] = jnp.where(col == 0, total[0], jnp.where(col == 1, total[1], jnp.where(col == 2, total[2], 0.0)))
    for t in range(FR):
        leave(t).wait()


VMEM = pl.BlockSpec(memory_space=pltpu.VMEM)
HBM = pl.BlockSpec(memory_space=pltpu.HBM)


def call(kernel, outs, *args, flops, scratch=(), limit=8 << 20, ins=None, places=None, aliases={}):
    return pl.pallas_call(
        kernel,
        out_shape=outs,
        in_specs=ins or [VMEM] * len(args),
        out_specs=places or jax.tree.map(lambda _: VMEM, outs),
        scratch_shapes=scratch,
        cost_estimate=pl.CostEstimate(flops=flops, bytes_accessed=1 << 20, transcendentals=0),
        compiler_params=pltpu.CompilerParams(vmem_limit_bytes=limit),
        input_output_aliases=aliases,
    )(*args)


def f32(*shape):
    return jax.ShapeDtypeStruct(shape, jnp.float32)


def both_ways(later, earlier, axis, ring=False):
    n = lax.axis_size(axis)
    pairs = [(i, (i + 1) % n) for i in range(n if ring else n - 1)]
    onward = lax.ppermute(later, axis, pairs)
    back = lax.ppermute(earlier, axis, [(b, a) for a, b in pairs])
    return onward, back


def spread_sum(part, axes):
    n = lax.axis_size(axes)
    rows = jnp.broadcast_to(part, (n, 128))
    return jnp.sum(lax.all_to_all(rows, axes, 0, 0, tiled=True), 0, keepdims=True)


def on_device(noisy, lam):
    n_tm, n_row, n_col = (lax.axis_size(a) for a in ("tm", "row", "col"))
    cells = float(noisy.size * n_tm * n_row * n_col)
    ext = lambda n: pltpu.VMEM((n, 3 * NTE + 1, 8, 128), jnp.float32)
    exto = lambda n: f32(n, 3 * NTE + 1, 8, 128)
    inner = lambda n: pltpu.VMEM((n, 128, 256), jnp.float32)
    strip, z, s_on, s_back, up, down, fv, lv = call(
        pack_kernel,
        (f32(NT, 8, 128), f32(16, 8, 128), f32(ZO + 10, 8, 128), f32(ZO + 10, 8, 128), f32(5, 128, 256), f32(5, 128, 256), f32(FR, 128, 256), f32(FR, 128, 256)),
        pltpu.with_memory_space_constraint(noisy, pltpu.HBM), pltpu.with_memory_space_constraint(lam, pltpu.HBM),
        flops=1 << 20, ins=[HBM, HBM], limit=8 << 20,
        scratch=[pltpu.SemaphoreType.DMA((2 * FR,))],
    )
    sp, sn = both_ways(s_on, s_back, "tm")
    bp, bn = both_ways(up, down, "tm")
    z_on, z_back = call(rows_kernel, (f32(NP, 8, 128), f32(NP, 8, 128)), z, sp, sn, flops=1 << 20)
    zp, zn = both_ways(z_on, z_back, "row")
    m = call(cols_kernel, f32(NTE, 8, 128), strip, sp, sn, zp, zn, flops=1 << 20)
    mp, mn = both_ways(m, m, "col", ring=True)
    sizes = (n_tm, n_row, n_col)
    *state, il, acc = call(
        functools.partial(prep_kernel, sizes),
        (exto(NF), exto(NF), exto(3 * NF), exto(NF), exto(NL), exto(NL), f32(12, 128, 256), f32(FR, 128, 256), f32(8, 128)),
        fv, lv, zp, zn, mp, mn,
        flops=1 << 24, limit=4 << 20,
    )
    out, part, *_ = call(
        functools.partial(main_kernel, sizes),
        (f32(4, 128, 256), f32(n_tm * n_col, 128), *(f32(*a.shape) for a in state)),
        fv, lv, bp, bn, il, acc, *state,
        flops=1 << 26, places=(HBM,) + (VMEM,) * 8,
        scratch=[ext(3 * NF), ext(NF), inner(12), inner(FR), pltpu.SemaphoreType.DMA((FR,))],
        aliases={6 + k: 2 + k for k in range(7)},
        limit=16 << 20,
    )
    part = jnp.sum(lax.all_to_all(part, ("tm", "col"), 0, 0, tiled=True), 0, keepdims=True)
    gaps = spread_sum(part, "row")[0, :3] / cells
    return out, gaps


def solution(mesh):
    spec = P("tm", "row", "col")
    return jax.shard_map(on_device, mesh=mesh, in_specs=(spec, spec), out_specs=(spec, P()), check_vma=False)
```

time: 92.7 us -> 91 us (0.982)
  waiting for transfers between devices: 15.7 us -> 14.7 us
    ppermute x4, waiting for transfers between devices: 5.98 us -> 4.93 us  [both_ways(): onward = lax.ppermute(later, axis, pairs)]
    pallas_call x4 -> x5, Pallas kernels: 12.2 us -> 11.8 us  [call(): pl.pallas_call(kernel, out_shape=outs, in_specs=ins or [VMEM] * len(args)...]
  transfers between devices with their start and end apart: 8 -> 8, of which waited for: 5 -> 5; matrix products, arithmetic and copies ran while one was open for 0% -> 0% of each run, Pallas kernels for 0% -> 3%
where the time goes in v3:
time: 91 us; the launch traced here: 90.7 us
  blocking collectives  40.1 us (44%)
  starting transfers between devices  22.8 us (25%)
  waiting for transfers between devices  14.7 us (16%)
  Pallas kernels  11.8 us (13%)
    all_to_all x1, blocking collectives, spread_sum(): lax.all_to_all(rows, axes, 0, 0, tiled=True)  25.9 us
    ppermute x4, starting transfers between devices, both_ways(): onward = lax.ppermute(later, axis, pairs)  15.9 us
    all_to_all x1, blocking collectives, on_device(): lax.all_to_all(part, ('tm', 'col'), 0, 0, tiled=True)  14.2 us
    pallas_call x5, Pallas kernels, call(): pl.pallas_call(kernel, out_shape=outs, in_specs=ins or [VMEM] * len(args)...  11.8 us
    ppermute x4, waiting for transfers between devices, both_ways(): back = lax.ppermute(earlier, axis, [(b, a) for a, b in pairs])  9.73 us
    ppermute x4, starting transfers between devices, both_ways(): back = lax.ppermute(earlier, axis, [(b, a) for a, b in pairs])  6.94 us
    ppermute x4, waiting for transfers between devices, both_ways(): onward = lax.ppermute(later, axis, pairs)  4.93 us
  transfers between devices with their start and end apart: 8, of which 5 were waited for; matrix products, arithmetic and copies ran while one was open for 0% of the time, Pallas kernels for 3%

profile of v3, /device:TPU:1, one launch (start us, length us, event | category | flops | bytes accessed | tf_op | source)
XLA Modules:
  0.0 90.7 jit_solution(4538101989165611290)
XLA Ops:
  0.6 1.6 %shard_map.41 = (f32[16,8,128]{2,1,0:T(8,128)S(1)}, f32[16,8,128]{2,1,0:T(8,128)S(1)}, f32[14,8,128]{2,1,0:T(8,128)S(1)}, f32[14,8,128]{2,1,0:T(8,128)S(1)}, f32...) custom-call(f32[4,128,256]{2,1,0:T(8,128)} %f_hbm.1, ...), custom_call_target="tpu_custom_call" | custom-call | flops 1048576 | bytes 1048576 | tf_op jit(solution)/shard_map/pallas_call | solution.py:400
  2.2 4.1 %collective-permute-start = (f32[5,128,256]{2,1,0:T(8,128)S(1)}, f32[5,128,256]{2,1,0:T(8,128)S(1)}, u32[]{:S(2)}, u32[]{:S(2)}) collective-permute-start(f32[5,128,256]{2,1,0:T(8,128)S(1)} %get-tuple-element.25), channel_id=1, source_target_pairs={{0,128},{128,256},{256,384},{1,129},{129,257},{257,385},{2,130},{1... | collective-permute-start | bytes 1966088 | tf_op jit(solution)/shard_map/ppermute | solution.py:419
  6.3 1.3 %collective-permute-start.1 = (f32[5,128,256]{2,1,0:T(8,128)S(1)}, f32[5,128,256]{2,1,0:T(8,128)S(1)}, u32[]{:S(2)}, u32[]{:S(2)}) collective-permute-start(f32[5,128,256]{2,1,0:T(8,128)S(1)} %get-tuple-element.26), channel_id=1, source_target_pairs={{128,0},{256,128},{384,256},{129,1},{257,129},{385,257},{130,2},{2... | collective-permute-start | bytes 1966088 | tf_op jit(solution)/shard_map/ppermute | solution.py:420
  7.6 4.0 %collective-permute-start.2 = (f32[14,8,128]{2,1,0:T(8,128)S(1)}, f32[14,8,128]{2,1,0:T(8,128)S(1)}, u32[]{:S(2)}, u32[]{:S(2)}) collective-permute-start(f32[14,8,128]{2,1,0:T(8,128)S(1)} %get-tuple-element.28), channel_id=1, source_target_pairs={{0,128},{128,256},{256,384},{1,129},{129,257},{257,385},{2,130},{1... | collective-permute-start | bytes 172040 | tf_op jit(solution)/shard_map/ppermute | solution.py:419
  11.6 1.3 %collective-permute-start.3 = (f32[14,8,128]{2,1,0:T(8,128)S(1)}, f32[14,8,128]{2,1,0:T(8,128)S(1)}, u32[]{:S(2)}, u32[]{:S(2)}) collective-permute-start(f32[14,8,128]{2,1,0:T(8,128)S(1)} %get-tuple-element.29), channel_id=1, source_target_pairs={{128,0},{256,128},{384,256},{129,1},{257,129},{385,257},{130,2},{2... | collective-permute-start | bytes 172040 | tf_op jit(solution)/shard_map/ppermute | solution.py:420
  12.9 4.8 %collective-permute-done.2.prev_ref = f32[14,8,128]{2,1,0:T(8,128)S(1)} collective-permute-done((f32[14,8,128]{2,1,0:T(8,128)S(1)}, f32[14,8,128]{2,1,0:T(8,128)S(1)}, u32[]{:S(2)}, u32[]{:S(2)}) %collective-permute-start.2) | collective-permute-done | bytes 57376 | tf_op jit(solution)/shard_map/ppermute | solution.py:419
  17.7 3.9 %collective-permute-done.3.next_ref = f32[14,8,128]{2,1,0:T(8,128)S(1)} collective-permute-done((f32[14,8,128]{2,1,0:T(8,128)S(1)}, f32[14,8,128]{2,1,0:T(8,128)S(1)}, u32[]{:S(2)}, u32[]{:S(2)}) %collective-permute-start.3) | collective-permute-done | bytes 57376 | tf_op jit(solution)/shard_map/ppermute | solution.py:420
  21.6 6.7 %collective-permute-start.4 = (f32[18,8,128]{2,1,0:T(8,128)S(1)}, f32[18,8,128]{2,1,0:T(8,128)S(1)}, u32[]{:S(2)}, u32[]{:S(2)}) collective-permute-start(f32[18,8,128]{2,1,0:T(8,128)S(1)} %get-tuple-element.30), channel_id=1, source_target_pairs={{0,8},{8,16},{16,24},{24,32},{32,40},{40,48},{48,56},{56,64},{64,7... | collective-permute-start | bytes 221192 | tf_op jit(solution)/shard_map/ppermute | solution.py:419
  28.3 1.3 %collective-permute-start.5 = (f32[18,8,128]{2,1,0:T(8,128)S(1)}, f32[18,8,128]{2,1,0:T(8,128)S(1)}, u32[]{:S(2)}, u32[]{:S(2)}) collective-permute-start(f32[18,8,128]{2,1,0:T(8,128)S(1)} %get-tuple-element.31), channel_id=1, source_target_pairs={{8,0},{16,8},{24,16},{32,24},{40,32},{48,40},{56,48},{64,56},{72,6... | collective-permute-start | bytes 221192 | tf_op jit(solution)/shard_map/ppermute | solution.py:420
  29.6 0.1 collective-permute-done.4.zp_ref
  29.7 3.9 %collective-permute-done.5.zn_ref = f32[18,8,128]{2,1,0:T(8,128)S(1)} collective-permute-done((f32[18,8,128]{2,1,0:T(8,128)S(1)}, f32[18,8,128]{2,1,0:T(8,128)S(1)}, u32[]{:S(2)}, u32[]{:S(2)}) %collective-permute-start.5) | collective-permute-done | bytes 73760 | tf_op jit(solution)/shard_map/ppermute | solution.py:420
  33.6 0.1 shard_map.43
  33.8 3.1 %collective-permute-start.7 = (f32[17,8,128]{2,1,0:T(8,128)S(1)}, f32[17,8,128]{2,1,0:T(8,128)S(1)}, u32[]{:S(2)}, u32[]{:S(2)}) collective-permute-start(f32[17,8,128]{2,1,0:T(8,128)S(1)} %shard_map.43), channel_id=1, source_target_pairs={{1,0},{2,1},{3,2},{4,3},{5,4},{6,5},{7,6},{0,7},{9,8},{10,9},{11,1... | collective-permute-start | bytes 208904 | tf_op jit(solution)/shard_map/ppermute | solution.py:420
  36.8 1.1 %collective-permute-start.6 = (f32[17,8,128]{2,1,0:T(8,128)S(1)}, f32[17,8,128]{2,1,0:T(8,128)S(1)}, u32[]{:S(2)}, u32[]{:S(2)}) collective-permute-start(f32[17,8,128]{2,1,0:T(8,128)S(1)} %shard_map.43), channel_id=1, source_target_pairs={{0,1},{1,2},{2,3},{3,4},{4,5},{5,6},{6,7},{7,0},{8,9},{9,10},{10,1... | collective-permute-start | bytes 208904 | tf_op jit(solution)/shard_map/ppermute | solution.py:419
  38.0 2.0 %collective-permute-done.7.mn_ref = f32[17,8,128]{2,1,0:T(8,128)S(1)} collective-permute-done((f32[17,8,128]{2,1,0:T(8,128)S(1)}, f32[17,8,128]{2,1,0:T(8,128)S(1)}, u32[]{:S(2)}, u32[]{:S(2)}) %collective-permute-start.7) | collective-permute-done | bytes 69664 | tf_op jit(solution)/shard_map/ppermute | solution.py:420
  39.9 0.0 collective-permute-done.6.mp_ref
  39.9 2.6 %shard_map.44 = (f32[10,52,8,128]{3,2,1,0:T(8,128)S(1)}, f32[10,52,8,128]{3,2,1,0:T(8,128)S(1)}, f32[30,52,8,128]{3,2,1,0:T(8,128)S(1)}, f32[10,52,8,128]{3,2,1,...) custom-call(f32[4,128,256]{2,1,0:T(8,128)S(1)} %get-tuple-element.23, ...), custom_call_target="tpu_custom_call" | custom-call | flops 16777216 | bytes 1048576 | tf_op jit(solution)/shard_map/pallas_call | solution.py:400
  42.6 0.0 collective-permute-done.bp_ref
  42.6 0.0 collective-permute-done.1.bn_ref
  42.6 7.4 %shard_map.45 = (f32[4,128,256]{2,1,0:T(8,128)}, f32[32,128]{1,0:T(8,128)S(1)}, f32[10,52,8,128]{3,2,1,0:T(8,128)S(1)}, f32[10,52,8,128]{3,2,1,0:T(8,128)S(1)}, ...) custom-call(f32[4,128,256]{2,1,0:T(8,128)S(1)} %get-tuple-element.23, ...), custom_call_target="tpu_custom_call", output_to_operand_aliasing={{2}: (6, {}), {3}: (7, {}), {4}: (8, {}), {5}: (9, {}), {6}... | custom-call | flops 67108864 | bytes 1048576 | tf_op jit(solution)/shard_map/pallas_call | solution.py:400
  50.0 14.2 %all_to_all.15 = f32[32,1,128]{2,1,0:T(1,128)S(1)} all-to-all(f32[32,1,128]{2,1,0:T(1,128)S(1)} %bitcast.7), channel_id=1, replica_groups=mesh['tm'=4,'row'=16,'col'=8] {'tm','col'}, dimensions={0} | all-to-all | bytes 32768 | tf_op jit(solution)/shard_map/all_to_all | solution.py:465
  64.2 0.1 reduce_sum.18
  64.2 25.9 %all_to_all.16 = f32[16,1,128]{2,1,0:T(1,128)S(1)} all-to-all(f32[16,1,128]{2,1,0:T(1,128)S(1)} %broadcast_in_dim.4), channel_id=1, replica_groups=mesh['tm'=4,'row'=16,'col'=8] {'row'}, dimensions={0} | all-to-all | bytes 16384 | tf_op jit(solution)/shard_map/all_to_all | solution.py:427
  90.1 0.5 multiply_bitcast_fusion
  (3 shorter events, 0.0 us)
Async XLA Ops:
  2.2 40.4 %collective-permute-start = (f32[5,128,256]{2,1,0:T(8,128)S(1)}, f32[5,128,256]{2,1,0:T(8,128)S(1)}, u32[]{:S(2)}, u32[]{:S(2)}) collective-permute-start(f32[5,128,256]{2,1,0:T(8,128)S(1)} %get-tuple-element.25), channel_id=1, source_target_pairs={{0,128},{128,256},{256,384},{1,129},{129,257},{257,385},{2,130},{1... | collective-permute-start | bytes 1966088 | tf_op jit(solution)/shard_map/ppermute | solution.py:419
  6.3 36.3 %collective-permute-start.1 = (f32[5,128,256]{2,1,0:T(8,128)S(1)}, f32[5,128,256]{2,1,0:T(8,128)S(1)}, u32[]{:S(2)}, u32[]{:S(2)}) collective-permute-start(f32[5,128,256]{2,1,0:T(8,128)S(1)} %get-tuple-element.26), channel_id=1, source_target_pairs={{128,0},{256,128},{384,256},{129,1},{257,129},{385,257},{130,2},{2... | collective-permute-start | bytes 1966088 | tf_op jit(solution)/shard_map/ppermute | solution.py:420
  7.6 10.1 %collective-permute-start.2 = (f32[14,8,128]{2,1,0:T(8,128)S(1)}, f32[14,8,128]{2,1,0:T(8,128)S(1)}, u32[]{:S(2)}, u32[]{:S(2)}) collective-permute-start(f32[14,8,128]{2,1,0:T(8,128)S(1)} %get-tuple-element.28), channel_id=1, source_target_pairs={{0,128},{128,256},{256,384},{1,129},{129,257},{257,385},{2,130},{1... | collective-permute-start | bytes 172040 | tf_op jit(solution)/shard_map/ppermute | solution.py:419
  11.6 10.0 %collective-permute-start.3 = (f32[14,8,128]{2,1,0:T(8,128)S(1)}, f32[14,8,128]{2,1,0:T(8,128)S(1)}, u32[]{:S(2)}, u32[]{:S(2)}) collective-permute-start(f32[14,8,128]{2,1,0:T(8,128)S(1)} %get-tuple-element.29), channel_id=1, source_target_pairs={{128,0},{256,128},{384,256},{129,1},{257,129},{385,257},{130,2},{2... | collective-permute-start | bytes 172040 | tf_op jit(solution)/shard_map/ppermute | solution.py:420
  21.6 8.1 %collective-permute-start.4 = (f32[18,8,128]{2,1,0:T(8,128)S(1)}, f32[18,8,128]{2,1,0:T(8,128)S(1)}, u32[]{:S(2)}, u32[]{:S(2)}) collective-permute-start(f32[18,8,128]{2,1,0:T(8,128)S(1)} %get-tuple-element.30), channel_id=1, source_target_pairs={{0,8},{8,16},{16,24},{24,32},{32,40},{40,48},{48,56},{56,64},{64,7... | collective-permute-start | bytes 221192 | tf_op jit(solution)/shard_map/ppermute | solution.py:419
  28.3 5.3 %collective-permute-start.5 = (f32[18,8,128]{2,1,0:T(8,128)S(1)}, f32[18,8,128]{2,1,0:T(8,128)S(1)}, u32[]{:S(2)}, u32[]{:S(2)}) collective-permute-start(f32[18,8,128]{2,1,0:T(8,128)S(1)} %get-tuple-element.31), channel_id=1, source_target_pairs={{8,0},{16,8},{24,16},{32,24},{40,32},{48,40},{56,48},{64,56},{72,6... | collective-permute-start | bytes 221192 | tf_op jit(solution)/shard_map/ppermute | solution.py:420
  33.8 6.2 %collective-permute-start.7 = (f32[17,8,128]{2,1,0:T(8,128)S(1)}, f32[17,8,128]{2,1,0:T(8,128)S(1)}, u32[]{:S(2)}, u32[]{:S(2)}) collective-permute-start(f32[17,8,128]{2,1,0:T(8,128)S(1)} %shard_map.43), channel_id=1, source_target_pairs={{1,0},{2,1},{3,2},{4,3},{5,4},{6,5},{7,6},{0,7},{9,8},{10,9},{11,1... | collective-permute-start | bytes 208904 | tf_op jit(solution)/shard_map/ppermute | solution.py:420
  36.8 3.1 %collective-permute-start.6 = (f32[17,8,128]{2,1,0:T(8,128)S(1)}, f32[17,8,128]{2,1,0:T(8,128)S(1)}, u32[]{:S(2)}, u32[]{:S(2)}) collective-permute-start(f32[17,8,128]{2,1,0:T(8,128)S(1)} %shard_map.43), channel_id=1, source_target_pairs={{0,1},{1,2},{2,3},{3,4},{4,5},{5,6},{6,7},{7,0},{8,9},{9,10},{10,1... | collective-permute-start | bytes 208904 | tf_op jit(solution)/shard_map/ppermute | solution.py:419

commit v4 on v3

--- a/solution.py
+++ b/solution.py
@@ -168,15 +168,16 @@
     row_mask = {NT - 1: jnp.where(sub == 7, ones * last_r, ones), NT: jnp.where(sub == 7, ones * first_r, ones)}
     col_mask = {1: jnp.where(lane == 127, ones * last_c, ones), 2: jnp.where(lane == 127, ones * first_c, ones)}
 
-    def dual_step(step, u, qi, qo, tt, gi, go, acc):
+    def dual_step(step, u, qi, qo, tt, gi, go, acc, js=(0, 1, 2), rows=NTE, kept=(0, 1, 2)):
         inside = acc is not None
         keep = jnp.where(((tt == 6) & last_t) | ((tt == 2) & first_t), zero, one)
-        here = [xtile(u, tt, 0, j) for j in range(3)]
+        near = sorted({j for j in js} | {(j + 1) % 3 for j in js})
+        here = {j: xtile(u, tt, 0, j) for j in near}
         start = here
-        for i in range(NTE):
-            after = start if i == NT else [xtile(u, tt, i + 1, j) for j in range(3)]
-            turned = [pltpu.roll(here[j], 127, 1) for j in range(3)]
-            for j in range(3):
+        for i in range(rows):
+            after = start if i == NT else {j: xtile(u, tt, i + 1, j) for j in near}
+            turned = {j: pltpu.roll(here[j], 127, 1) for j in near}
+            for j in js:
                 x = here[j]
                 d0 = (xtile(u, tt + 1, i, j) - x) * keep
                 d1 = pltpu.roll(jnp.where(sub == 0, after[j], x), 7, 0) - x
@@ -199,7 +200,7 @@
                 m = d if step == 0 else tuple(d[k] + xtile(qi, NF * k + tt, i, j) for k in range(3))
                 n2 = (m[0] * m[0] + m[1] * m[1] + m[2] * m[2]) * (SIG * SIG)
                 s = jnp.minimum(1.0, lax.rsqrt(n2))
-                for k in range(3):
+                for k in kept:
                     xput(qo, NF * k + tt, i, j, m[k] * s)
             here = after
 
@@ -236,8 +237,8 @@
     return dual_step, primal_step
 
 
-def prep_kernel(sizes, f_ref, l_ref, zp_ref, zn_ref, mp_ref, mn_ref, ua, ub, qa, v1, wt, at, g1, il, acc_ref):
-    sub, lane = iota(0), iota(1)
+def fill_kernel(sizes, f_ref, l_ref, zp_ref, zn_ref, ua, qa, wt, at, g1, il):
+    sub = iota(0)
 
     def fill_noisy(src, at0, dst):
         for i in range(NT):
@@ -266,6 +267,19 @@
                 w, a = prim(z, xtile(ua, p - NF + 1, NT, j))
                 xput(wt, p - NF, NT, j, w)
                 xput(at, p - NF, NT, j, a)
+
+    dual_step, _ = steps_of(sizes, f_ref, l_ref, wt, at, il, None)
+
+    def dual_in(tt, c):
+        dual_step(0, ua, None, qa, tt, None, g1, [None] * 2, js=(0,))
+        return c
+
+    lax.fori_loop(3, 6, dual_in, 0)
+
+
+def prep_kernel(sizes, f_ref, l_ref, mp_ref, mn_ref, il, *refs):
+    (ub, v1, acc_ref, ua, qa, wt, at, g1) = refs[5:]
+    lane = iota(1)
 
     from_left = lane % LW < 3
     beside = (lane < 3) | (lane >= 125)
@@ -289,7 +303,7 @@
     dual_step, primal_step = steps_of(sizes, f_ref, l_ref, wt, at, il, None)
 
     def dual_in(tt, c):
-        dual_step(0, ua, None, qa, tt, None, g1, list(c))
+        dual_step(0, ua, None, qa, tt, None, g1, [None] * 2, js=(1, 2))
         return c
 
     def primal_in(tt, c):
@@ -298,7 +312,7 @@
         return tuple(acc)
 
     blank = jnp.zeros((8, 128), jnp.float32)
-    lax.fori_loop(3, 6, dual_in, (blank, blank))
+    lax.fori_loop(3, 6, dual_in, 0)
     acc = lax.fori_loop(4, 6, primal_in, (blank, blank))
     acc_ref[...] = acc[0] + acc[1]
 
@@ -345,6 +359,12 @@
         def dual_out(k, c):
             dual_step(step, u, qi, qo, jnp.where(k < 3, k, k + 4), gi, go, None)
             return c
+
+        def dual_first():
+            if step == 2:
+                dual_step(step, u, qi, qo, lo, gi, go, None, js=(0, 1), rows=NT, kept=(0,))
+            else:
+                dual_step(step, u, qi, qo, lo, gi, go, None, kept=(0,))
 
         def dual_in(tt, c):
             acc = list(c)
@@ -364,7 +384,9 @@
             return tuple(acc)
 
         blank = jnp.zeros((8, 128), jnp.float32)
-        lax.fori_loop(lo, hi - 3, dual_out, 0)
+        dual_first()
+        if step < 2:
+            lax.fori_loop(lo + 1, hi - 3, dual_out, 0)
         acc = lax.fori_loop(6 if step == 0 else 3, 7, dual_in, (blank, blank))
         if step < 2:
             lax.fori_loop(lo + 1, hi - 3, primal_out, 0)
@@ -447,12 +469,19 @@
     m = call(cols_kernel, f32(NTE, 8, 128), strip, sp, sn, zp, zn, flops=1 << 20)
     mp, mn = both_ways(m, m, "col", ring=True)
     sizes = (n_tm, n_row, n_col)
-    *state, il, acc = call(
+    ua, qa, wt, at, g1, il = call(
+        functools.partial(fill_kernel, sizes),
+        (exto(NF), exto(3 * NF), exto(NL), exto(NL), f32(12, 128, 256), f32(FR, 128, 256)),
+        fv, lv, zp, zn,
+        flops=1 << 22, limit=4 << 20,
+    )
+    ub, v1, acc, ua, qa, wt, at, g1 = call(
         functools.partial(prep_kernel, sizes),
-        (exto(NF), exto(NF), exto(3 * NF), exto(NF), exto(NL), exto(NL), f32(12, 128, 256), f32(FR, 128, 256), f32(8, 128)),
-        fv, lv, zp, zn, mp, mn,
-        flops=1 << 24, limit=4 << 20,
+        (exto(NF), exto(NF), f32(8, 128), *(f32(*a.shape) for a in (ua, qa, wt, at, g1))),
+        fv, lv, mp, mn, il, ua, qa, wt, at, g1,
+        flops=1 << 24, limit=4 << 20, aliases={5 + k: 3 + k for k in range(5)},
     )
+    state = (ua, ub, qa, v1, wt, at, g1)
     out, part, *_ = call(
         functools.partial(main_kernel, sizes),
         (f32(4, 128, 256), f32(n_tm * n_col, 128), *(f32(*a.shape) for a in state)),

time: 91 us -> 90.5 us (level)
    pallas_call x5 -> x6, Pallas kernels: 11.8 us -> 11.9 us  [call(): pl.pallas_call(kernel, out_shape=outs, in_specs=ins or [VMEM] * len(args)...]
where the time goes in v4:
time: 90.5 us; the launch traced here: 90.2 us
  blocking collectives  40.1 us (44%)
  starting transfers between devices  22.8 us (25%)
  waiting for transfers between devices  14.1 us (16%)
  Pallas kernels  11.9 us (13%)
    all_to_all x1, blocking collectives, spread_sum(): lax.all_to_all(rows, axes, 0, 0, tiled=True)  25.9 us
    ppermute x4, starting transfers between devices, both_ways(): onward = lax.ppermute(later, axis, pairs)  15.9 us
    all_to_all x1, blocking collectives, on_device(): lax.all_to_all(part, ('tm', 'col'), 0, 0, tiled=True)  14.2 us
    pallas_call x6, Pallas kernels, call(): pl.pallas_call(kernel, out_shape=outs, in_specs=ins or [VMEM] * len(args)...  11.9 us
    ppermute x4, waiting for transfers between devices, both_ways(): back = lax.ppermute(earlier, axis, [(b, a) for a, b in pairs])  9.16 us
    ppermute x4, starting transfers between devices, both_ways(): back = lax.ppermute(earlier, axis, [(b, a) for a, b in pairs])  6.94 us
    ppermute x4, waiting for transfers between devices, both_ways(): onward = lax.ppermute(later, axis, pairs)  4.93 us
  transfers between devices with their start and end apart: 8, of which 5 were waited for; matrix products, arithmetic and copies ran while one was open for 0% of the time, Pallas kernels for 3%

profile of v4, /device:TPU:1, one launch (start us, length us, event | category | flops | bytes accessed | tf_op | source)
XLA Modules:
  0.0 90.2 jit_solution(9620499353668689636)
XLA Ops:
  0.6 1.6 %shard_map.41 = (f32[16,8,128]{2,1,0:T(8,128)S(1)}, f32[16,8,128]{2,1,0:T(8,128)S(1)}, f32[14,8,128]{2,1,0:T(8,128)S(1)}, f32[14,8,128]{2,1,0:T(8,128)S(1)}, f32...) custom-call(f32[4,128,256]{2,1,0:T(8,128)} %f_hbm.1, ...), custom_call_target="tpu_custom_call" | custom-call | flops 1048576 | bytes 1048576 | tf_op jit(solution)/shard_map/pallas_call | solution.py:422
  2.2 4.1 %collective-permute-start = (f32[5,128,256]{2,1,0:T(8,128)S(1)}, f32[5,128,256]{2,1,0:T(8,128)S(1)}, u32[]{:S(2)}, u32[]{:S(2)}) collective-permute-start(f32[5,128,256]{2,1,0:T(8,128)S(1)} %get-tuple-element.30), channel_id=1, source_target_pairs={{0,128},{128,256},{256,384},{1,129},{129,257},{257,385},{2,130},{1... | collective-permute-start | bytes 1966088 | tf_op jit(solution)/shard_map/ppermute | solution.py:441
  6.3 1.3 %collective-permute-start.1 = (f32[5,128,256]{2,1,0:T(8,128)S(1)}, f32[5,128,256]{2,1,0:T(8,128)S(1)}, u32[]{:S(2)}, u32[]{:S(2)}) collective-permute-start(f32[5,128,256]{2,1,0:T(8,128)S(1)} %get-tuple-element.31), channel_id=1, source_target_pairs={{128,0},{256,128},{384,256},{129,1},{257,129},{385,257},{130,2},{2... | collective-permute-start | bytes 1966088 | tf_op jit(solution)/shard_map/ppermute | solution.py:442
  7.6 4.0 %collective-permute-start.2 = (f32[14,8,128]{2,1,0:T(8,128)S(1)}, f32[14,8,128]{2,1,0:T(8,128)S(1)}, u32[]{:S(2)}, u32[]{:S(2)}) collective-permute-start(f32[14,8,128]{2,1,0:T(8,128)S(1)} %get-tuple-element.33), channel_id=1, source_target_pairs={{0,128},{128,256},{256,384},{1,129},{129,257},{257,385},{2,130},{1... | collective-permute-start | bytes 172040 | tf_op jit(solution)/shard_map/ppermute | solution.py:441
  11.6 1.3 %collective-permute-start.3 = (f32[14,8,128]{2,1,0:T(8,128)S(1)}, f32[14,8,128]{2,1,0:T(8,128)S(1)}, u32[]{:S(2)}, u32[]{:S(2)}) collective-permute-start(f32[14,8,128]{2,1,0:T(8,128)S(1)} %get-tuple-element.34), channel_id=1, source_target_pairs={{128,0},{256,128},{384,256},{129,1},{257,129},{385,257},{130,2},{2... | collective-permute-start | bytes 172040 | tf_op jit(solution)/shard_map/ppermute | solution.py:442
  12.9 4.8 %collective-permute-done.2.prev_ref = f32[14,8,128]{2,1,0:T(8,128)S(1)} collective-permute-done((f32[14,8,128]{2,1,0:T(8,128)S(1)}, f32[14,8,128]{2,1,0:T(8,128)S(1)}, u32[]{:S(2)}, u32[]{:S(2)}) %collective-permute-start.2) | collective-permute-done | bytes 57376 | tf_op jit(solution)/shard_map/ppermute | solution.py:441
  17.7 3.9 %collective-permute-done.3.next_ref = f32[14,8,128]{2,1,0:T(8,128)S(1)} collective-permute-done((f32[14,8,128]{2,1,0:T(8,128)S(1)}, f32[14,8,128]{2,1,0:T(8,128)S(1)}, u32[]{:S(2)}, u32[]{:S(2)}) %collective-permute-start.3) | collective-permute-done | bytes 57376 | tf_op jit(solution)/shard_map/ppermute | solution.py:442
  21.6 6.7 %collective-permute-start.4 = (f32[18,8,128]{2,1,0:T(8,128)S(1)}, f32[18,8,128]{2,1,0:T(8,128)S(1)}, u32[]{:S(2)}, u32[]{:S(2)}) collective-permute-start(f32[18,8,128]{2,1,0:T(8,128)S(1)} %get-tuple-element.35), channel_id=1, source_target_pairs={{0,8},{8,16},{16,24},{24,32},{32,40},{40,48},{48,56},{56,64},{64,7... | collective-permute-start | bytes 221192 | tf_op jit(solution)/shard_map/ppermute | solution.py:441
  28.3 1.3 %collective-permute-start.5 = (f32[18,8,128]{2,1,0:T(8,128)S(1)}, f32[18,8,128]{2,1,0:T(8,128)S(1)}, u32[]{:S(2)}, u32[]{:S(2)}) collective-permute-start(f32[18,8,128]{2,1,0:T(8,128)S(1)} %get-tuple-element.36), channel_id=1, source_target_pairs={{8,0},{16,8},{24,16},{32,24},{40,32},{48,40},{56,48},{64,56},{72,6... | collective-permute-start | bytes 221192 | tf_op jit(solution)/shard_map/ppermute | solution.py:442
  29.6 0.1 collective-permute-done.4.zp_ref
  29.7 3.9 %collective-permute-done.5.zn_ref = f32[18,8,128]{2,1,0:T(8,128)S(1)} collective-permute-done((f32[18,8,128]{2,1,0:T(8,128)S(1)}, f32[18,8,128]{2,1,0:T(8,128)S(1)}, u32[]{:S(2)}, u32[]{:S(2)}) %collective-permute-start.5) | collective-permute-done | bytes 73760 | tf_op jit(solution)/shard_map/ppermute | solution.py:442
  33.6 0.1 shard_map.44
  33.8 3.1 %collective-permute-start.7 = (f32[17,8,128]{2,1,0:T(8,128)S(1)}, f32[17,8,128]{2,1,0:T(8,128)S(1)}, u32[]{:S(2)}, u32[]{:S(2)}) collective-permute-start(f32[17,8,128]{2,1,0:T(8,128)S(1)} %shard_map.44), channel_id=1, source_target_pairs={{1,0},{2,1},{3,2},{4,3},{5,4},{6,5},{7,6},{0,7},{9,8},{10,9},{11,1... | collective-permute-start | bytes 208904 | tf_op jit(solution)/shard_map/ppermute | solution.py:442
  36.8 1.1 %collective-permute-start.6 = (f32[17,8,128]{2,1,0:T(8,128)S(1)}, f32[17,8,128]{2,1,0:T(8,128)S(1)}, u32[]{:S(2)}, u32[]{:S(2)}) collective-permute-start(f32[17,8,128]{2,1,0:T(8,128)S(1)} %shard_map.44), channel_id=1, source_target_pairs={{0,1},{1,2},{2,3},{3,4},{4,5},{5,6},{6,7},{7,0},{8,9},{9,10},{10,1... | collective-permute-start | bytes 208904 | tf_op jit(solution)/shard_map/ppermute | solution.py:441
  38.0 0.6 shard_map.43
  38.5 1.4 %collective-permute-done.7.mn_ref = f32[17,8,128]{2,1,0:T(8,128)S(1)} collective-permute-done((f32[17,8,128]{2,1,0:T(8,128)S(1)}, f32[17,8,128]{2,1,0:T(8,128)S(1)}, u32[]{:S(2)}, u32[]{:S(2)}) %collective-permute-start.7) | collective-permute-done | bytes 69664 | tf_op jit(solution)/shard_map/ppermute | solution.py:442
  39.9 0.0 collective-permute-done.6.mp_ref
  39.9 2.3 %shard_map.45 = (f32[10,52,8,128]{3,2,1,0:T(8,128)S(1)}, f32[10,52,8,128]{3,2,1,0:T(8,128)S(1)}, f32[8,128]{1,0:T(8,128)S(1)}, f32[10,52,8,128]{3,2,1,0:T(8,128)...) custom-call(f32[4,128,256]{2,1,0:T(8,128)S(1)} %get-tuple-element.28, ...), custom_call_target="tpu_custom_call", output_to_operand_aliasing={{3}: (5, {}), {4}: (6, {}), {5}: (7, {}), {6}: (8, {}), {7}... | custom-call | flops 16777216 | bytes 1048576 | tf_op jit(solution)/shard_map/pallas_call | solution.py:422
  42.2 0.0 collective-permute-done.bp_ref
  42.2 0.0 collective-permute-done.1.bn_ref
  42.3 7.3 %shard_map.46 = (f32[4,128,256]{2,1,0:T(8,128)}, f32[32,128]{1,0:T(8,128)S(1)}, f32[10,52,8,128]{3,2,1,0:T(8,128)S(1)}, f32[10,52,8,128]{3,2,1,0:T(8,128)S(1)}, ...) custom-call(f32[4,128,256]{2,1,0:T(8,128)S(1)} %get-tuple-element.28, ...), custom_call_target="tpu_custom_call", output_to_operand_aliasing={{2}: (6, {}), {3}: (7, {}), {4}: (8, {}), {5}: (9, {}), {6}... | custom-call | flops 67108864 | bytes 1048576 | tf_op jit(solution)/shard_map/pallas_call | solution.py:422
  49.5 14.2 %all_to_all.15 = f32[32,1,128]{2,1,0:T(1,128)S(1)} all-to-all(f32[32,1,128]{2,1,0:T(1,128)S(1)} %bitcast.7), channel_id=1, replica_groups=mesh['tm'=4,'row'=16,'col'=8] {'tm','col'}, dimensions={0} | all-to-all | bytes 32768 | tf_op jit(solution)/shard_map/all_to_all | solution.py:494
  63.7 0.1 reduce_sum.18
  63.8 25.9 %all_to_all.16 = f32[16,1,128]{2,1,0:T(1,128)S(1)} all-to-all(f32[16,1,128]{2,1,0:T(1,128)S(1)} %broadcast_in_dim.4), channel_id=1, replica_groups=mesh['tm'=4,'row'=16,'col'=8] {'row'}, dimensions={0} | all-to-all | bytes 16384 | tf_op jit(solution)/shard_map/all_to_all | solution.py:449
  89.7 0.5 multiply_bitcast_fusion
  (3 shorter events, 0.0 us)
Async XLA Ops:
  2.2 40.0 %collective-permute-start = (f32[5,128,256]{2,1,0:T(8,128)S(1)}, f32[5,128,256]{2,1,0:T(8,128)S(1)}, u32[]{:S(2)}, u32[]{:S(2)}) collective-permute-start(f32[5,128,256]{2,1,0:T(8,128)S(1)} %get-tuple-element.30), channel_id=1, source_target_pairs={{0,128},{128,256},{256,384},{1,129},{129,257},{257,385},{2,130},{1... | collective-permute-start | bytes 1966088 | tf_op jit(solution)/shard_map/ppermute | solution.py:441
  6.3 35.9 %collective-permute-start.1 = (f32[5,128,256]{2,1,0:T(8,128)S(1)}, f32[5,128,256]{2,1,0:T(8,128)S(1)}, u32[]{:S(2)}, u32[]{:S(2)}) collective-permute-start(f32[5,128,256]{2,1,0:T(8,128)S(1)} %get-tuple-element.31), channel_id=1, source_target_pairs={{128,0},{256,128},{384,256},{129,1},{257,129},{385,257},{130,2},{2... | collective-permute-start | bytes 1966088 | tf_op jit(solution)/shard_map/ppermute | solution.py:442
  7.6 10.1 %collective-permute-start.2 = (f32[14,8,128]{2,1,0:T(8,128)S(1)}, f32[14,8,128]{2,1,0:T(8,128)S(1)}, u32[]{:S(2)}, u32[]{:S(2)}) collective-permute-start(f32[14,8,128]{2,1,0:T(8,128)S(1)} %get-tuple-element.33), channel_id=1, source_target_pairs={{0,128},{128,256},{256,384},{1,129},{129,257},{257,385},{2,130},{1... | collective-permute-start | bytes 172040 | tf_op jit(solution)/shard_map/ppermute | solution.py:441
  11.6 10.0 %collective-permute-start.3 = (f32[14,8,128]{2,1,0:T(8,128)S(1)}, f32[14,8,128]{2,1,0:T(8,128)S(1)}, u32[]{:S(2)}, u32[]{:S(2)}) collective-permute-start(f32[14,8,128]{2,1,0:T(8,128)S(1)} %get-tuple-element.34), channel_id=1, source_target_pairs={{128,0},{256,128},{384,256},{129,1},{257,129},{385,257},{130,2},{2... | collective-permute-start | bytes 172040 | tf_op jit(solution)/shard_map/ppermute | solution.py:442
  21.6 8.1 %collective-permute-start.4 = (f32[18,8,128]{2,1,0:T(8,128)S(1)}, f32[18,8,128]{2,1,0:T(8,128)S(1)}, u32[]{:S(2)}, u32[]{:S(2)}) collective-permute-start(f32[18,8,128]{2,1,0:T(8,128)S(1)} %get-tuple-element.35), channel_id=1, source_target_pairs={{0,8},{8,16},{16,24},{24,32},{32,40},{40,48},{48,56},{56,64},{64,7... | collective-permute-start | bytes 221192 | tf_op jit(solution)/shard_map/ppermute | solution.py:441
  28.3 5.3 %collective-permute-start.5 = (f32[18,8,128]{2,1,0:T(8,128)S(1)}, f32[18,8,128]{2,1,0:T(8,128)S(1)}, u32[]{:S(2)}, u32[]{:S(2)}) collective-permute-start(f32[18,8,128]{2,1,0:T(8,128)S(1)} %get-tuple-element.36), channel_id=1, source_target_pairs={{8,0},{16,8},{24,16},{32,24},{40,32},{48,40},{56,48},{64,56},{72,6... | collective-permute-start | bytes 221192 | tf_op jit(solution)/shard_map/ppermute | solution.py:442
  33.8 6.2 %collective-permute-start.7 = (f32[17,8,128]{2,1,0:T(8,128)S(1)}, f32[17,8,128]{2,1,0:T(8,128)S(1)}, u32[]{:S(2)}, u32[]{:S(2)}) collective-permute-start(f32[17,8,128]{2,1,0:T(8,128)S(1)} %shard_map.44), channel_id=1, source_target_pairs={{1,0},{2,1},{3,2},{4,3},{5,4},{6,5},{7,6},{0,7},{9,8},{10,9},{11,1... | collective-permute-start | bytes 208904 | tf_op jit(solution)/shard_map/ppermute | solution.py:442
  36.8 3.1 %collective-permute-start.6 = (f32[17,8,128]{2,1,0:T(8,128)S(1)}, f32[17,8,128]{2,1,0:T(8,128)S(1)}, u32[]{:S(2)}, u32[]{:S(2)}) collective-permute-start(f32[17,8,128]{2,1,0:T(8,128)S(1)} %shard_map.44), channel_id=1, source_target_pairs={{0,1},{1,2},{2,3},{3,4},{4,5},{5,6},{6,7},{7,0},{8,9},{9,10},{10,1... | collective-permute-start | bytes 208904 | tf_op jit(solution)/shard_map/ppermute | solution.py:441

commit v5 on v4

--- a/solution.py
+++ b/solution.py
@@ -41,7 +41,7 @@
 
 
 def size_of(square):
-    return square * lax.rsqrt(jnp.maximum(square, 1e-37))
+    return square * lax.rsqrt(jnp.maximum(square, 1.1754944e-38))
 
 
 def strip_of(lane, acc, p, first, last):
@@ -170,7 +170,7 @@
 
     def dual_step(step, u, qi, qo, tt, gi, go, acc, js=(0, 1, 2), rows=NTE, kept=(0, 1, 2)):
         inside = acc is not None
-        keep = jnp.where(((tt == 6) & last_t) | ((tt == 2) & first_t), zero, one)
+        onward = jnp.where(((tt == 6) & last_t) | ((tt == 2) & first_t), tt, tt + 1)
         near = sorted({j for j in js} | {(j + 1) % 3 for j in js})
         here = {j: xtile(u, tt, 0, j) for j in near}
         start = here
@@ -178,8 +178,13 @@
             after = start if i == NT else {j: xtile(u, tt, i + 1, j) for j in near}
             turned = {j: pltpu.roll(here[j], 127, 1) for j in near}
             for j in js:
+                need = kept
+                if inside and step == 2:
+                    if i == NT and j == 2:
+                        continue
+                    need = (1,) if i == NT else (2,) if j == 2 else kept
                 x = here[j]
-                d0 = (xtile(u, tt + 1, i, j) - x) * keep
+                d0 = xtile(u, onward, i, j) - x
                 d1 = pltpu.roll(jnp.where(sub == 0, after[j], x), 7, 0) - x
                 if i in row_mask:
                     d1 = d1 * row_mask[i]
@@ -200,7 +205,7 @@
                 m = d if step == 0 else tuple(d[k] + xtile(qi, NF * k + tt, i, j) for k in range(3))
                 n2 = (m[0] * m[0] + m[1] * m[1] + m[2] * m[2]) * (SIG * SIG)
                 s = jnp.minimum(1.0, lax.rsqrt(n2))
-                for k in kept:
+                for k in need:
                     xput(qo, NF * k + tt, i, j, m[k] * s)
             here = after
 

time: 90.5 us -> 90.3 us (level)
  no operation moved by 1% of the time
where the time goes in v5:
time: 90.3 us; the launch traced here: 90 us
  blocking collectives  40.1 us (44%)
  starting transfers between devices  22.8 us (25%)
  waiting for transfers between devices  14.1 us (16%)
  Pallas kernels  11.7 us (13%)
    all_to_all x1, blocking collectives, spread_sum(): lax.all_to_all(rows, axes, 0, 0, tiled=True)  25.9 us
    ppermute x4, starting transfers between devices, both_ways(): onward = lax.ppermute(later, axis, pairs)  15.9 us
    all_to_all x1, blocking collectives, on_device(): lax.all_to_all(part, ('tm', 'col'), 0, 0, tiled=True)  14.2 us
    pallas_call x6, Pallas kernels, call(): pl.pallas_call(kernel, out_shape=outs, in_specs=ins or [VMEM] * len(args)...  11.7 us
    ppermute x4, waiting for transfers between devices, both_ways(): back = lax.ppermute(earlier, axis, [(b, a) for a, b in pairs])  9.16 us
    ppermute x4, starting transfers between devices, both_ways(): back = lax.ppermute(earlier, axis, [(b, a) for a, b in pairs])  6.94 us
    ppermute x4, waiting for transfers between devices, both_ways(): onward = lax.ppermute(later, axis, pairs)  4.93 us
  transfers between devices with their start and end apart: 8, of which 5 were waited for; matrix products, arithmetic and copies ran while one was open for 0% of the time, Pallas kernels for 3%

profile of v5, /device:TPU:1, one launch (start us, length us, event | category | flops | bytes accessed | tf_op | source)
XLA Modules:
  0.0 90.0 jit_solution(12156489785806562409)
XLA Ops:
  0.6 1.6 %shard_map.41 = (f32[16,8,128]{2,1,0:T(8,128)S(1)}, f32[16,8,128]{2,1,0:T(8,128)S(1)}, f32[14,8,128]{2,1,0:T(8,128)S(1)}, f32[14,8,128]{2,1,0:T(8,128)S(1)}, f32...) custom-call(f32[4,128,256]{2,1,0:T(8,128)} %f_hbm.1, ...), custom_call_target="tpu_custom_call" | custom-call | flops 1048576 | bytes 1048576 | tf_op jit(solution)/shard_map/pallas_call | solution.py:427
  2.2 4.1 %collective-permute-start = (f32[5,128,256]{2,1,0:T(8,128)S(1)}, f32[5,128,256]{2,1,0:T(8,128)S(1)}, u32[]{:S(2)}, u32[]{:S(2)}) collective-permute-start(f32[5,128,256]{2,1,0:T(8,128)S(1)} %get-tuple-element.30), channel_id=1, source_target_pairs={{0,128},{128,256},{256,384},{1,129},{129,257},{257,385},{2,130},{1... | collective-permute-start | bytes 1966088 | tf_op jit(solution)/shard_map/ppermute | solution.py:446
  6.3 1.3 %collective-permute-start.1 = (f32[5,128,256]{2,1,0:T(8,128)S(1)}, f32[5,128,256]{2,1,0:T(8,128)S(1)}, u32[]{:S(2)}, u32[]{:S(2)}) collective-permute-start(f32[5,128,256]{2,1,0:T(8,128)S(1)} %get-tuple-element.31), channel_id=1, source_target_pairs={{128,0},{256,128},{384,256},{129,1},{257,129},{385,257},{130,2},{2... | collective-permute-start | bytes 1966088 | tf_op jit(solution)/shard_map/ppermute | solution.py:447
  7.6 4.0 %collective-permute-start.2 = (f32[14,8,128]{2,1,0:T(8,128)S(1)}, f32[14,8,128]{2,1,0:T(8,128)S(1)}, u32[]{:S(2)}, u32[]{:S(2)}) collective-permute-start(f32[14,8,128]{2,1,0:T(8,128)S(1)} %get-tuple-element.33), channel_id=1, source_target_pairs={{0,128},{128,256},{256,384},{1,129},{129,257},{257,385},{2,130},{1... | collective-permute-start | bytes 172040 | tf_op jit(solution)/shard_map/ppermute | solution.py:446
  11.6 1.3 %collective-permute-start.3 = (f32[14,8,128]{2,1,0:T(8,128)S(1)}, f32[14,8,128]{2,1,0:T(8,128)S(1)}, u32[]{:S(2)}, u32[]{:S(2)}) collective-permute-start(f32[14,8,128]{2,1,0:T(8,128)S(1)} %get-tuple-element.34), channel_id=1, source_target_pairs={{128,0},{256,128},{384,256},{129,1},{257,129},{385,257},{130,2},{2... | collective-permute-start | bytes 172040 | tf_op jit(solution)/shard_map/ppermute | solution.py:447
  12.9 4.8 %collective-permute-done.2.prev_ref = f32[14,8,128]{2,1,0:T(8,128)S(1)} collective-permute-done((f32[14,8,128]{2,1,0:T(8,128)S(1)}, f32[14,8,128]{2,1,0:T(8,128)S(1)}, u32[]{:S(2)}, u32[]{:S(2)}) %collective-permute-start.2) | collective-permute-done | bytes 57376 | tf_op jit(solution)/shard_map/ppermute | solution.py:446
  17.7 3.9 %collective-permute-done.3.next_ref = f32[14,8,128]{2,1,0:T(8,128)S(1)} collective-permute-done((f32[14,8,128]{2,1,0:T(8,128)S(1)}, f32[14,8,128]{2,1,0:T(8,128)S(1)}, u32[]{:S(2)}, u32[]{:S(2)}) %collective-permute-start.3) | collective-permute-done | bytes 57376 | tf_op jit(solution)/shard_map/ppermute | solution.py:447
  21.6 6.7 %collective-permute-start.4 = (f32[18,8,128]{2,1,0:T(8,128)S(1)}, f32[18,8,128]{2,1,0:T(8,128)S(1)}, u32[]{:S(2)}, u32[]{:S(2)}) collective-permute-start(f32[18,8,128]{2,1,0:T(8,128)S(1)} %get-tuple-element.35), channel_id=1, source_target_pairs={{0,8},{8,16},{16,24},{24,32},{32,40},{40,48},{48,56},{56,64},{64,7... | collective-permute-start | bytes 221192 | tf_op jit(solution)/shard_map/ppermute | solution.py:446
  28.3 1.3 %collective-permute-start.5 = (f32[18,8,128]{2,1,0:T(8,128)S(1)}, f32[18,8,128]{2,1,0:T(8,128)S(1)}, u32[]{:S(2)}, u32[]{:S(2)}) collective-permute-start(f32[18,8,128]{2,1,0:T(8,128)S(1)} %get-tuple-element.36), channel_id=1, source_target_pairs={{8,0},{16,8},{24,16},{32,24},{40,32},{48,40},{56,48},{64,56},{72,6... | collective-permute-start | bytes 221192 | tf_op jit(solution)/shard_map/ppermute | solution.py:447
  29.6 0.1 collective-permute-done.4.zp_ref
  29.7 3.9 %collective-permute-done.5.zn_ref = f32[18,8,128]{2,1,0:T(8,128)S(1)} collective-permute-done((f32[18,8,128]{2,1,0:T(8,128)S(1)}, f32[18,8,128]{2,1,0:T(8,128)S(1)}, u32[]{:S(2)}, u32[]{:S(2)}) %collective-permute-start.5) | collective-permute-done | bytes 73760 | tf_op jit(solution)/shard_map/ppermute | solution.py:447
  33.6 0.1 shard_map.44
  33.8 3.1 %collective-permute-start.7 = (f32[17,8,128]{2,1,0:T(8,128)S(1)}, f32[17,8,128]{2,1,0:T(8,128)S(1)}, u32[]{:S(2)}, u32[]{:S(2)}) collective-permute-start(f32[17,8,128]{2,1,0:T(8,128)S(1)} %shard_map.44), channel_id=1, source_target_pairs={{1,0},{2,1},{3,2},{4,3},{5,4},{6,5},{7,6},{0,7},{9,8},{10,9},{11,1... | collective-permute-start | bytes 208904 | tf_op jit(solution)/shard_map/ppermute | solution.py:447
  36.8 1.1 %collective-permute-start.6 = (f32[17,8,128]{2,1,0:T(8,128)S(1)}, f32[17,8,128]{2,1,0:T(8,128)S(1)}, u32[]{:S(2)}, u32[]{:S(2)}) collective-permute-start(f32[17,8,128]{2,1,0:T(8,128)S(1)} %shard_map.44), channel_id=1, source_target_pairs={{0,1},{1,2},{2,3},{3,4},{4,5},{5,6},{6,7},{7,0},{8,9},{9,10},{10,1... | collective-permute-start | bytes 208904 | tf_op jit(solution)/shard_map/ppermute | solution.py:446
  38.0 0.6 shard_map.43
  38.5 1.4 %collective-permute-done.7.mn_ref = f32[17,8,128]{2,1,0:T(8,128)S(1)} collective-permute-done((f32[17,8,128]{2,1,0:T(8,128)S(1)}, f32[17,8,128]{2,1,0:T(8,128)S(1)}, u32[]{:S(2)}, u32[]{:S(2)}) %collective-permute-start.7) | collective-permute-done | bytes 69664 | tf_op jit(solution)/shard_map/ppermute | solution.py:447
  39.9 0.0 collective-permute-done.6.mp_ref
  39.9 2.3 %shard_map.45 = (f32[10,52,8,128]{3,2,1,0:T(8,128)S(1)}, f32[10,52,8,128]{3,2,1,0:T(8,128)S(1)}, f32[8,128]{1,0:T(8,128)S(1)}, f32[10,52,8,128]{3,2,1,0:T(8,128)...) custom-call(f32[4,128,256]{2,1,0:T(8,128)S(1)} %get-tuple-element.28, ...), custom_call_target="tpu_custom_call", output_to_operand_aliasing={{3}: (5, {}), {4}: (6, {}), {5}: (7, {}), {6}: (8, {}), {7}... | custom-call | flops 16777216 | bytes 1048576 | tf_op jit(solution)/shard_map/pallas_call | solution.py:427
  42.2 0.0 collective-permute-done.bp_ref
  42.3 0.0 collective-permute-done.1.bn_ref
  42.3 7.1 %shard_map.46 = (f32[4,128,256]{2,1,0:T(8,128)}, f32[32,128]{1,0:T(8,128)S(1)}, f32[10,52,8,128]{3,2,1,0:T(8,128)S(1)}, f32[10,52,8,128]{3,2,1,0:T(8,128)S(1)}, ...) custom-call(f32[4,128,256]{2,1,0:T(8,128)S(1)} %get-tuple-element.28, ...), custom_call_target="tpu_custom_call", output_to_operand_aliasing={{2}: (6, {}), {3}: (7, {}), {4}: (8, {}), {5}: (9, {}), {6}... | custom-call | flops 67108864 | bytes 1048576 | tf_op jit(solution)/shard_map/pallas_call | solution.py:427
  49.3 14.2 %all_to_all.15 = f32[32,1,128]{2,1,0:T(1,128)S(1)} all-to-all(f32[32,1,128]{2,1,0:T(1,128)S(1)} %bitcast.7), channel_id=1, replica_groups=mesh['tm'=4,'row'=16,'col'=8] {'tm','col'}, dimensions={0} | all-to-all | bytes 32768 | tf_op jit(solution)/shard_map/all_to_all | solution.py:499
  63.5 0.1 reduce_sum.18
  63.6 25.9 %all_to_all.16 = f32[16,1,128]{2,1,0:T(1,128)S(1)} all-to-all(f32[16,1,128]{2,1,0:T(1,128)S(1)} %broadcast_in_dim.4), channel_id=1, replica_groups=mesh['tm'=4,'row'=16,'col'=8] {'row'}, dimensions={0} | all-to-all | bytes 16384 | tf_op jit(solution)/shard_map/all_to_all | solution.py:454
  89.5 0.5 multiply_bitcast_fusion
  (3 shorter events, 0.0 us)
Async XLA Ops:
  2.2 40.0 %collective-permute-start = (f32[5,128,256]{2,1,0:T(8,128)S(1)}, f32[5,128,256]{2,1,0:T(8,128)S(1)}, u32[]{:S(2)}, u32[]{:S(2)}) collective-permute-start(f32[5,128,256]{2,1,0:T(8,128)S(1)} %get-tuple-element.30), channel_id=1, source_target_pairs={{0,128},{128,256},{256,384},{1,129},{129,257},{257,385},{2,130},{1... | collective-permute-start | bytes 1966088 | tf_op jit(solution)/shard_map/ppermute | solution.py:446
  6.3 36.0 %collective-permute-start.1 = (f32[5,128,256]{2,1,0:T(8,128)S(1)}, f32[5,128,256]{2,1,0:T(8,128)S(1)}, u32[]{:S(2)}, u32[]{:S(2)}) collective-permute-start(f32[5,128,256]{2,1,0:T(8,128)S(1)} %get-tuple-element.31), channel_id=1, source_target_pairs={{128,0},{256,128},{384,256},{129,1},{257,129},{385,257},{130,2},{2... | collective-permute-start | bytes 1966088 | tf_op jit(solution)/shard_map/ppermute | solution.py:447
  7.6 10.1 %collective-permute-start.2 = (f32[14,8,128]{2,1,0:T(8,128)S(1)}, f32[14,8,128]{2,1,0:T(8,128)S(1)}, u32[]{:S(2)}, u32[]{:S(2)}) collective-permute-start(f32[14,8,128]{2,1,0:T(8,128)S(1)} %get-tuple-element.33), channel_id=1, source_target_pairs={{0,128},{128,256},{256,384},{1,129},{129,257},{257,385},{2,130},{1... | collective-permute-start | bytes 172040 | tf_op jit(solution)/shard_map/ppermute | solution.py:446
  11.6 10.0 %collective-permute-start.3 = (f32[14,8,128]{2,1,0:T(8,128)S(1)}, f32[14,8,128]{2,1,0:T(8,128)S(1)}, u32[]{:S(2)}, u32[]{:S(2)}) collective-permute-start(f32[14,8,128]{2,1,0:T(8,128)S(1)} %get-tuple-element.34), channel_id=1, source_target_pairs={{128,0},{256,128},{384,256},{129,1},{257,129},{385,257},{130,2},{2... | collective-permute-start | bytes 172040 | tf_op jit(solution)/shard_map/ppermute | solution.py:447
  21.6 8.1 %collective-permute-start.4 = (f32[18,8,128]{2,1,0:T(8,128)S(1)}, f32[18,8,128]{2,1,0:T(8,128)S(1)}, u32[]{:S(2)}, u32[]{:S(2)}) collective-permute-start(f32[18,8,128]{2,1,0:T(8,128)S(1)} %get-tuple-element.35), channel_id=1, source_target_pairs={{0,8},{8,16},{16,24},{24,32},{32,40},{40,48},{48,56},{56,64},{64,7... | collective-permute-start | bytes 221192 | tf_op jit(solution)/shard_map/ppermute | solution.py:446
  28.3 5.3 %collective-permute-start.5 = (f32[18,8,128]{2,1,0:T(8,128)S(1)}, f32[18,8,128]{2,1,0:T(8,128)S(1)}, u32[]{:S(2)}, u32[]{:S(2)}) collective-permute-start(f32[18,8,128]{2,1,0:T(8,128)S(1)} %get-tuple-element.36), channel_id=1, source_target_pairs={{8,0},{16,8},{24,16},{32,24},{40,32},{48,40},{56,48},{64,56},{72,6... | collective-permute-start | bytes 221192 | tf_op jit(solution)/shard_map/ppermute | solution.py:447
  33.8 6.2 %collective-permute-start.7 = (f32[17,8,128]{2,1,0:T(8,128)S(1)}, f32[17,8,128]{2,1,0:T(8,128)S(1)}, u32[]{:S(2)}, u32[]{:S(2)}) collective-permute-start(f32[17,8,128]{2,1,0:T(8,128)S(1)} %shard_map.44), channel_id=1, source_target_pairs={{1,0},{2,1},{3,2},{4,3},{5,4},{6,5},{7,6},{0,7},{9,8},{10,9},{11,1... | collective-permute-start | bytes 208904 | tf_op jit(solution)/shard_map/ppermute | solution.py:447
  36.8 3.1 %collective-permute-start.6 = (f32[17,8,128]{2,1,0:T(8,128)S(1)}, f32[17,8,128]{2,1,0:T(8,128)S(1)}, u32[]{:S(2)}, u32[]{:S(2)}) collective-permute-start(f32[17,8,128]{2,1,0:T(8,128)S(1)} %shard_map.44), channel_id=1, source_target_pairs={{0,1},{1,2},{2,3},{3,4},{4,5},{5,6},{6,7},{7,0},{8,9},{9,10},{10,1... | collective-permute-start | bytes 208904 | tf_op jit(solution)/shard_map/ppermute | solution.py:446
